TPU v7x, 128 devices: a whole 4x4x4 slice. The times are simulated.
128 devices in a mesh: tp: 4 (over x), dp: 32 (over z, y, core).
Axes of the slice: x: 4, y: 4, z: 4, core: 2. Of those that a mesh axis runs over, the one named last changes fastest.
Arguments:
- tokens: int32 [64, 1536], P('dp')
- cotangent: bfloat16 [64, 1536, 1024], P('dp')
- emb_table: bfloat16 [50304, 1024], P('tp')
- w_qkv: bfloat16 [1024, 3072], P(None, 'tp')
- b_qkv: bfloat16 [16, 192], P('tp')
- w_out: bfloat16 [1024, 1024], P('tp')
- b_out: bfloat16 [1024], replicated
- ln1_gain: bfloat16 [1024], replicated
- ln1_bias: bfloat16 [1024], replicated
- w_gate: bfloat16 [1024, 4096], P(None, 'tp')
- b_gate: bfloat16 [4096], P('tp')
- w_lin: bfloat16 [1024, 4096], P(None, 'tp')
- b_lin: bfloat16 [4096], P('tp')
- w_down: bfloat16 [4096, 1024], P('tp')
- b_down: bfloat16 [1024], replicated
- ln2_gain: bfloat16 [1024], replicated
Outputs:
- output 1: float32 [50304, 1024], P('tp')
- output 2: float32 [1024, 3072], P(None, 'tp')
- output 3: float32 [16, 192], P('tp')
- output 4: float32 [1024, 1024], P('tp')
- output 5: float32 [1024], replicated
- output 6: float32 [1024], replicated
- output 7: float32 [1024], replicated
- output 8: float32 [1024, 4096], P(None, 'tp')
- output 9: float32 [4096], P('tp')
- output 10: float32 [1024, 4096], P(None, 'tp')
- output 11: float32 [4096], P('tp')
- output 12: float32 [4096, 1024], P('tp')
- output 13: float32 [1024], replicated
- output 14: float32 [1024], replicated
All inputs are finite; a program needn't handle non-finite values.
Results may differ from a plain program's by a relative error of at most 0.0152027.
Values sent between devices are 32-bit elements.
A program may use at most 1 GiB of HBM per device.

v0:
```python
import functools

import jax
import jax.numpy as jnp
from jax import lax
from jax.experimental import pallas as pl
from jax.experimental.pallas import tpu as pltpu
from jax.sharding import Mesh, PartitionSpec as P


ALPHA = 140.0 ** 0.5
EPS = 1e-5
SHRINK = 0.1
ROPE_BASE = 10000.0
F32 = jnp.float32
BF16 = jnp.bfloat16
SWAP = ((0, 1), (1, 0))


def swap(values):
    return lax.ppermute(values, 'c', SWAP)


def unit():
    return 1.0 + (lax.axis_index('x') // lax.axis_size('x')).astype(F32)


def rounded(values):
    return (values * unit()).astype(BF16)


def norm_scaled(values, gain):
    mean_val = jnp.mean(values, axis=-1, keepdims=True)
    centered = values - mean_val
    variance = jnp.mean(centered * centered, axis=-1, keepdims=True)
    return centered * lax.rsqrt(variance + EPS) * gain


def dot(left, right):
    return jnp.dot(left, right, preferred_element_type=F32)


def dot_tn(left, right):
    return lax.dot_general(left, right, (((0,), (0,)), ((), ())), preferred_element_type=F32)


def dot_nt(left, right):
    return lax.dot_general(left, right, (((1,), (1,)), ((), ())), preferred_element_type=F32)


def rope_tables(seq_len, head_dim):
    half_dim = head_dim // 2
    inv_freq = ROPE_BASE ** (-2.0 * jnp.arange(half_dim, dtype=F32) / head_dim)
    angles = jnp.arange(seq_len, dtype=F32)[:, None] * inv_freq[None, :]
    cos, sin = jnp.cos(angles), jnp.sin(angles)
    return jnp.concatenate([cos, cos, cos, cos], axis=1), jnp.concatenate([-sin, sin, -sin, sin], axis=1)


def lanes_of_head(rows, head):
    lane = lax.broadcasted_iota(jnp.int32, (rows, 128), 1)
    return (lane >= 64) if head else (lane < 64)


def rotate(values):
    lane = lax.broadcasted_iota(jnp.int32, values.shape, 1)
    return jnp.where(lane % 64 < 32, pltpu.roll(values, 96, axis=1), pltpu.roll(values, 32, axis=1))


def only_head(values, head):
    return jnp.where(lanes_of_head(values.shape[0], head), values, jnp.zeros_like(values))


def stage_qkv(core, half, qkv_ref, cos_ref, sin_ref, q_scr, k_scr, v_scr):
    for part in (0, 1):
        local = pl.ds(part * half, half)
        place = pl.ds(pl.multiple_of((core * half + part * half) % (2 * half), half), half)
        cos, sin = cos_ref[place, :], sin_ref[place, :]
        q = qkv_ref[local, 0:128].astype(F32)
        k = qkv_ref[local, 128:256].astype(F32)
        q_scr[place, :] = (q * cos + rotate(q) * sin).astype(BF16) * BF16(0.125)
        k_scr[place, :] = (k * cos + rotate(k) * sin).astype(BF16)
        v_scr[place, :] = qkv_ref[local, 256:384]


def softmax_rows(q_h, k_scr, row0, rows):
    s_diag = dot_nt(q_h, k_scr[row0:row0 + rows, :])
    keep = lax.broadcasted_iota(jnp.int32, (rows, rows), 0) >= lax.broadcasted_iota(jnp.int32, (rows, rows), 1)
    scores = jnp.where(keep, s_diag, -1e30)
    if row0:
        scores = jnp.concatenate([dot_nt(q_h, k_scr[0:row0, :]), scores], axis=1)
    top = jnp.max(scores, axis=1, keepdims=True)
    weights = jnp.exp(scores - top)
    total = jnp.sum(weights, axis=1, keepdims=True)
    return (weights * (1.0 / total)).astype(BF16)


def attn_fwd_kernel(half, rows, core_ref, qkv_ref, cos_ref, sin_ref, ctx_ref, q_scr, k_scr, v_scr, ctx_scr):
    core = core_ref[0]
    seq_len = 2 * half
    stage_qkv(core, half, qkv_ref, cos_ref, sin_ref, q_scr, k_scr, v_scr)
    for row0 in range(0, seq_len, rows):
        q_blk = q_scr[row0:row0 + rows, :]
        v_blk = v_scr[0:row0 + rows, :]
        ctx = jnp.zeros((rows, 128), F32)
        for head in (0, 1):
            probs = softmax_rows(only_head(q_blk, head), k_scr, row0, rows)
            ctx = jnp.where(lanes_of_head(rows, head), dot(probs, v_blk), ctx)
        ctx_scr[row0:row0 + rows, :] = ctx.astype(BF16)
    for part in (0, 1):
        place = pl.ds(pl.multiple_of((core * half + part * half) % seq_len, half), half)
        ctx_ref[part * half:(part + 1) * half, :] = ctx_scr[place, :]


def attn_bwd_kernel(half, rows, core_ref, qkv_ref, dctx_ref, cos_ref, sin_ref, dqkv_ref, dbias_ref,
                    q_scr, k_scr, v_scr, do_scr, dq_scr, dk_scr, dv_scr):
    core = core_ref[0]
    seq_len = 2 * half
    stage_qkv(core, half, qkv_ref, cos_ref, sin_ref, q_scr, k_scr, v_scr)
    for part in (0, 1):
        place = pl.ds(pl.multiple_of((core * half + part * half) % seq_len, half), half)
        do_scr[place, :] = dctx_ref[part * half:(part + 1) * half, :]
    dk_scr[...] = jnp.zeros_like(dk_scr)
    dv_scr[...] = jnp.zeros_like(dv_scr)
    for row0 in range(0, seq_len, rows):
        end = row0 + rows
        q_blk = q_scr[row0:end, :]
        do_blk = do_scr[row0:end, :]
        k_blk = k_scr[0:end, :]
        v_blk = v_scr[0:end, :]
        dq = jnp.zeros((rows, 128), F32)
        for head in (0, 1):
            q_h = only_head(q_blk, head)
            do_h = only_head(do_blk, head)
            probs = softmax_rows(q_h, k_scr, row0, rows)
            d_probs = dot_nt(do_h, v_blk)
            probs_f = probs.astype(F32)
            inner = jnp.sum(d_probs * probs_f, axis=1, keepdims=True)
            d_scores = (probs_f * (d_probs - inner)).astype(BF16)
            dq = jnp.where(lanes_of_head(rows, head), dot(d_scores, k_blk), dq)
            dk_scr[0:end, :] += dot_tn(d_scores, q_h)
            dv_scr[0:end, :] += dot_tn(probs, do_h)
        dq_scr[row0:end, :] = dq * 0.125
    for part in (0, 1):
        place = pl.ds(pl.multiple_of((core * half + part * half) % seq_len, half), half)
        cos, sin = cos_ref[place, :], -sin_ref[place, :]
        dq, dk, dv = dq_scr[place, :], dk_scr[place, :], dv_scr[place, :]
        dq = dq * cos + rotate(dq) * sin
        dk = dk * cos + rotate(dk) * sin
        for place_out, grad in ((0, dq), (128, dk), (256, dv)):
            dqkv_ref[part * half:(part + 1) * half, place_out:place_out + 128] = grad.astype(BF16)
            total = jnp.sum(grad, axis=0, keepdims=True)
            if part:
                dbias_ref[0:1, place_out:place_out + 128] += total
            else:
                dbias_ref[0:1, place_out:place_out + 128] = total


def attention_forward(core, qkv, cos_tab, sin_tab, rows):
    seq_len, width = qkv.shape
    pairs = width // 384
    full = pl.BlockSpec((seq_len, 128), lambda p, c: (0, 0))
    return pl.pallas_call(
        functools.partial(attn_fwd_kernel, seq_len // 2, rows),
        grid_spec=pltpu.PrefetchScalarGridSpec(
            num_scalar_prefetch=1,
            grid=(pairs,),
            in_specs=[pl.BlockSpec((seq_len, 384), lambda p, c: (0, p)), full, full],
            out_specs=pl.BlockSpec((seq_len, 128), lambda p, c: (0, p)),
            scratch_shapes=[pltpu.VMEM((seq_len, 128), BF16)] * 4,
        ),
        out_shape=jax.ShapeDtypeStruct((seq_len, pairs * 128), BF16),
        compiler_params=pltpu.CompilerParams(vmem_limit_bytes=48 * 1024 * 1024),
        cost_estimate=pl.CostEstimate(flops=seq_len * seq_len * 128 * 4 * pairs, bytes_accessed=seq_len * width * 3, transcendentals=seq_len * seq_len * pairs),
        name='attn_fwd',
    )(core, qkv, cos_tab, sin_tab)


def attention_backward(core, qkv, d_ctx, cos_tab, sin_tab, rows):
    seq_len, width = qkv.shape
    pairs = width // 384
    full = pl.BlockSpec((seq_len, 128), lambda p, c: (0, 0))
    return pl.pallas_call(
        functools.partial(attn_bwd_kernel, seq_len // 2, rows),
        grid_spec=pltpu.PrefetchScalarGridSpec(
            num_scalar_prefetch=1,
            grid=(pairs,),
            in_specs=[pl.BlockSpec((seq_len, 384), lambda p, c: (0, p)), pl.BlockSpec((seq_len, 128), lambda p, c: (0, p)), full, full],
            out_specs=[pl.BlockSpec((seq_len, 384), lambda p, c: (0, p)), pl.BlockSpec((1, 384), lambda p, c: (0, p))],
            scratch_shapes=[pltpu.VMEM((seq_len, 128), BF16)] * 4 + [pltpu.VMEM((seq_len, 128), F32)] * 3,
        ),
        out_shape=[jax.ShapeDtypeStruct((seq_len, width), BF16), jax.ShapeDtypeStruct((1, width), F32)],
        compiler_params=pltpu.CompilerParams(vmem_limit_bytes=56 * 1024 * 1024),
        cost_estimate=pl.CostEstimate(flops=seq_len * seq_len * 128 * 10 * pairs, bytes_accessed=seq_len * width * 5, transcendentals=seq_len * seq_len * pairs),
        name='attn_bwd',
    )(core, qkv, d_ctx, cos_tab, sin_tab)


def geglu_fwd_kernel(chunk, hidden_ref, wide_ref, bias_ref, inner_ref, act_ref, slope_ref, weight_ref):
    rows, cols = inner_ref.shape
    weight_ref[...] = wide_ref[...].reshape(weight_ref.shape).astype(BF16)
    for row0 in range(0, rows, chunk):
        place = slice(row0, row0 + chunk)
        part = hidden_ref[place, :]
        gate = dot_nt(part, weight_ref[0:cols, :]) + bias_ref[:, 0:cols]
        lin = dot_nt(part, weight_ref[cols:2 * cols, :]) + bias_ref[:, cols:2 * cols]
        below = 0.5 + 0.5 * lax.erf(gate * (0.5 ** 0.5))
        act = gate * below
        act_ref[place, :] = act
        slope_ref[place, :] = (below + gate * jnp.exp(gate * gate * -0.5) * ((2.0 * jnp.pi) ** -0.5)) * lin
        inner_ref[place, :] = (act * lin).astype(BF16)


def geglu_forward(hidden, weight, bias, groups):
    seq_len, width = hidden.shape
    slices, _, slice_rows, _ = weight.shape
    cols = slices * slice_rows // 2
    tile = pl.BlockSpec((seq_len, cols), lambda i: (0, i))
    shape = (seq_len, groups * cols)
    return pl.pallas_call(
        functools.partial(geglu_fwd_kernel, min(256, seq_len)),
        grid=(groups,),
        in_specs=[pl.BlockSpec((seq_len, width), lambda i: (0, 0)), pl.BlockSpec((slices, 1, slice_rows, width), lambda i: (0, i, 0, 0)), pl.BlockSpec((1, 2 * cols), lambda i: (0, i))],
        out_specs=[tile, tile, tile, pl.BlockSpec((2 * cols, width), lambda i: (i, 0))],
        out_shape=[jax.ShapeDtypeStruct(shape, BF16), jax.ShapeDtypeStruct(shape, F32), jax.ShapeDtypeStruct(shape, F32), jax.ShapeDtypeStruct((2 * shape[1], width), BF16)],
        compiler_params=pltpu.CompilerParams(vmem_limit_bytes=56 * 1024 * 1024),
        cost_estimate=pl.CostEstimate(flops=4 * seq_len * width * shape[1], bytes_accessed=seq_len * shape[1] * 10, transcendentals=2 * seq_len * shape[1]),
        name='geglu_fwd',
    )(hidden, weight, bias)


def geglu_bwd_kernel(chunk, d_ffn_ref, weight_ref, act_ref, slope_ref, grad_ref, sum_ref):
    rows, cols = act_ref.shape
    for row0 in range(0, rows, chunk):
        place = slice(row0, row0 + chunk)
        d_inner = dot_nt(d_ffn_ref[place, :], weight_ref[...]).astype(BF16).astype(F32)
        for at, factor in ((0, slope_ref), (cols, act_ref)):
            grad = d_inner * factor[place, :]
            grad_ref[place, at:at + cols] = grad.astype(BF16)
            total = jnp.sum(grad, axis=0, keepdims=True)
            if row0:
                sum_ref[:, at:at + cols] += total
            else:
                sum_ref[:, at:at + cols] = total


def geglu_backward(d_ffn, weight, act, slope, groups):
    seq_len, width = d_ffn.shape
    cols = weight.shape[0] // groups
    tile = pl.BlockSpec((seq_len, cols), lambda i: (0, i))
    return pl.pallas_call(
        functools.partial(geglu_bwd_kernel, min(256, seq_len)),
        grid=(groups,),
        in_specs=[pl.BlockSpec((seq_len, width), lambda i: (0, 0)), pl.BlockSpec((cols, width), lambda i: (i, 0)), tile, tile],
        out_specs=[pl.BlockSpec((seq_len, 2 * cols), lambda i: (0, i)), pl.BlockSpec((1, 2 * cols), lambda i: (0, i))],
        out_shape=[jax.ShapeDtypeStruct((seq_len, 2 * groups * cols), BF16), jax.ShapeDtypeStruct((1, 2 * groups * cols), F32)],
        compiler_params=pltpu.CompilerParams(vmem_limit_bytes=56 * 1024 * 1024),
        cost_estimate=pl.CostEstimate(flops=2 * seq_len * width * groups * cols, bytes_accessed=seq_len * groups * cols * 12, transcendentals=0),
        name='geglu_bwd',
    )(d_ffn, weight, act, slope)


def bucket_kernel(streams, group_ref, value_ref, list_ref, count_ref):
    size = group_ref.shape[0] // streams
    for slot in range(streams * 5):
        count_ref[slot] = 0

    def place(step, carry):
        spots = []
        for stream in range(streams):
            group = group_ref[stream * size + step]
            spots.append((stream * 5 + group, value_ref[stream * size + step]))
        filled = [count_ref[slot] for slot, _ in spots]
        for (slot, value), at in zip(spots, filled):
            list_ref[slot * size + at] = value
            count_ref[slot] = at + 1
        return carry

    lax.fori_loop(0, size, place, 0)


def bucket_ids(ids, streams, vocab):
    total = ids.shape[0]
    size = total // streams
    span = vocab // 4
    group = jnp.where(ids < 0, 4, ids // span)
    value = jnp.where(ids < 0, 0, (ids % span) * total + jnp.arange(total, dtype=jnp.int32))
    smem = pl.BlockSpec(memory_space=pltpu.SMEM)
    return pl.pallas_call(
        functools.partial(bucket_kernel, streams),
        in_specs=[smem, smem],
        out_specs=[smem, smem],
        out_shape=[jax.ShapeDtypeStruct((streams * 5 * size,), jnp.int32), jax.ShapeDtypeStruct((streams * 5,), jnp.int32)],
        cost_estimate=pl.CostEstimate(flops=40_000_000, bytes_accessed=20 * total, transcendentals=0),
        name='bucket_ids',
    )(group, value)


def table_kernel(total, streams, list_ref, count_ref, *refs):
    blocks, out_ref, rows, bufs, in_sem, out_sem = refs[:-5], refs[-5], refs[-4], refs[-3], refs[-2], refs[-1]
    span, width = bufs.shape[1:]
    loads = []
    first = 0
    for index, block in enumerate(blocks):
        loads.append(pltpu.make_async_copy(block, rows.at[pl.ds(first, block.shape[0]), :], in_sem.at[index]))
        first += block.shape[0]
    for load in loads:
        load.start()

    def store(group):
        return pltpu.make_async_copy(bufs.at[group % 2], out_ref.at[pl.ds(group * span, span), :], out_sem.at[group % 2])

    for group in range(4):
        buf = bufs.at[group % 2]
        if group >= 2:
            store(group - 2).wait()

        def clear(step, carry):
            buf[pl.ds(pl.multiple_of(step * 8, 8), 8), :] = jnp.zeros((8, width), F32)
            return carry

        lax.fori_loop(0, span // 8, clear, 0, unroll=3 if (span // 8) % 3 == 0 else 1)
        if group == 0:
            for load in loads:
                load.wait()

        for stream in range(streams):
            slot = stream * 5 + group
            base = slot * (total // streams)

            def add_row(index):
                packed = list_ref[base + index]
                target = packed // total
                source = packed - target * total
                buf[pl.ds(target, 1), :] += rows[pl.ds(source, 1), :]

            def add_four(step, carry):
                for k in range(4):
                    add_row(step * 4 + k)
                return carry

            def add_one(index, carry):
                add_row(index)
                return carry

            count = count_ref[slot]
            lax.fori_loop(0, count // 4, add_four, 0)
            lax.fori_loop(count // 4 * 4, count, add_one, 0)
        store(group).start()
    store(2).wait()
    store(3).wait()


def add_rows(lists, counts, blocks, vocab):
    width = blocks[0].shape[1]
    total = sum(block.shape[0] for block in blocks)
    return pl.pallas_call(
        functools.partial(table_kernel, total, counts.shape[0] // 5),
        grid_spec=pltpu.PrefetchScalarGridSpec(
            num_scalar_prefetch=2,
            grid=(),
            in_specs=[pl.BlockSpec(memory_space=pl.ANY)] * len(blocks),
            out_specs=pl.BlockSpec(memory_space=pl.ANY),
            scratch_shapes=[pltpu.VMEM((total, width), F32), pltpu.VMEM((2, vocab // 4, width), F32), pltpu.SemaphoreType.DMA((len(blocks),)), pltpu.SemaphoreType.DMA((2,))],
        ),
        out_shape=jax.ShapeDtypeStruct((vocab, width), F32),
        compiler_params=pltpu.CompilerParams(vmem_limit_bytes=44 * 1024 * 1024),
        cost_estimate=pl.CostEstimate(flops=30 * vocab * width, bytes_accessed=4 * vocab * width, transcendentals=0),
        name='table_rows',
    )(lists, counts, *blocks)


def ring_blocks(values, axis, n, split=True):
    if n == 1:
        return [(0, values)]
    right = [(i, (i + 1) % n) for i in range(n)]
    left = [(i, (i - 1) % n) for i in range(n)]
    if n == 2:
        return [(0, values), (1, lax.ppermute(values, axis, right))]
    from_left, from_right = lax.ppermute(values, axis, right), lax.ppermute(values, axis, left)
    mid = values.shape[0] // 2
    if split:
        far = jnp.concatenate([lax.ppermute(from_left[:mid], axis, right), lax.ppermute(from_right[mid:], axis, left)], axis=0)
    else:
        far = lax.ppermute(values, axis, [(i, (i + 2) % n) for i in range(n)])
    return [(0, values), (-1, from_left), (1, from_right), (2, far)]


def in_order(blocks, axis, n):
    if n == 1:
        return blocks[0][1][None]
    whole = jnp.zeros((n,) + blocks[0][1].shape, blocks[0][1].dtype)
    for offset, block in blocks:
        whole = lax.dynamic_update_index_in_dim(whole, block, (lax.axis_index(axis) + offset) % n, 0)
    return whole


def pair_order(rows, n_pairs):
    split = rows.reshape(n_pairs, 2, 3, 64, *rows.shape[1:])
    return jnp.swapaxes(split, 1, 2).reshape(rows.shape)


def head_order(rows, n_pairs):
    split = rows.reshape(n_pairs, 3, 2, 64, *rows.shape[1:])
    return jnp.swapaxes(split, 1, 2).reshape(rows.shape)


def solution(mesh):
    n_tp = mesh.shape['tp']
    n_dp = mesh.shape['dp']
    n_q = n_dp // 2
    n_z = 4 if n_q >= 16 else n_q
    n_y = n_q // n_z
    fine = Mesh(mesh.devices.reshape(n_tp, n_z, n_y, 2), ('x', 'z', 'y', 'c'))
    col, row, rep, vec = P(None, 'x'), P('x', None), P(), P('x')
    weight_specs = (col, row, row, rep, rep, rep, col, vec, col, vec, row, rep, rep)
    in_specs = (P(('z', 'y', 'c'), None), P(('z', 'y', 'c'), None, None), row) + weight_specs
    out_specs = (row,) + weight_specs

    def device_step(tokens, cotangent, emb_table, w_qkv, b_qkv, w_out, b_out, ln1_gain, ln1_bias, w_gate, b_gate, w_lin, b_lin, w_down, b_down, ln2_gain):
        xi, ci = lax.axis_index('x'), lax.axis_index('c')
        qi = lax.axis_index(('z', 'y'))
        seqs, seq_len = tokens.shape
        half = seq_len // 2
        vocab_loc, width = emb_table.shape
        heads_loc = b_qkv.shape[0]
        pairs_loc = heads_loc // 4

        def half_of(values, which, axis):
            size = values.shape[axis] // 2
            return lax.dynamic_slice_in_dim(values, which * size, size, axis)

        def share(values, axis):
            size = values.shape[axis] // n_q
            return lax.dynamic_slice_in_dim(values, qi * size, size, axis)

        qkv_cols = w_qkv.shape[1] // 2
        ffn_cols = w_gate.shape[1] // 2
        bias_rows = jnp.concatenate([
            pair_order(half_of(b_qkv.astype(F32), ci, 0).reshape(-1), pairs_loc),
            half_of(b_gate.astype(F32), ci, 0), half_of(b_lin.astype(F32), ci, 0)])
        bias_rows = jnp.pad(bias_rows, (0, -bias_rows.shape[0] % (8 * width))).reshape(-1, width)
        gate_lin = jnp.concatenate([half_of(w_gate, ci, 1), half_of(w_lin, ci, 1)], axis=1)
        parts = [
            share(pair_order(half_of(w_qkv, ci, 1).T, pairs_loc), 0),
            share(half_of(w_out, ci, 0), 0),
            share(gate_lin, 1).T]
        starts = [bias_rows.shape[0]]
        for part in parts:
            starts.append(starts[-1] + part.shape[0])
        packed = jnp.concatenate([bias_rows] + [part.astype(F32) for part in parts], axis=0)
        packed_blocks = ring_blocks(packed, 'x', n_tp, split=False)

        other_tokens = swap(tokens)
        line_tokens = jnp.where(ci == 0, jnp.concatenate([tokens, other_tokens], axis=0), jnp.concatenate([other_tokens, tokens], axis=0)) - xi * vocab_loc
        line_ids = half_of(line_tokens, ci, 1)
        in_shard = (line_ids >= 0) & (line_ids < vocab_loc)
        safe_ids = jnp.where(in_shard, line_ids, 0)
        right = [(i, (i + 1) % n_tp) for i in range(n_tp)]
        left = [(i, (i - 1) % n_tp) for i in range(n_tp)]
        quarter = half // 2
        steps = jnp.arange(1, n_tp + 1, dtype=jnp.int32)
        ring_ids = jnp.stack([
            jnp.take(safe_ids[:, :quarter], (xi - steps) % n_tp, axis=0),
            jnp.take(safe_ids[:, quarter:], (xi + steps) % n_tp, axis=0)], axis=1)
        ring_here = jnp.stack([
            jnp.take(in_shard[:, :quarter], (xi - steps) % n_tp, axis=0),
            jnp.take(in_shard[:, quarter:], (xi + steps) % n_tp, axis=0)], axis=1)
        first_ids, later_ids = ring_ids[:1].reshape(-1), ring_ids[1:].reshape(-1)
        first = emb_table.at[first_ids].get(mode='promise_in_bounds')
        offsets = [offset for offset, _ in packed_blocks]
        first, later_ids, packed_values = lax.optimization_barrier((first, later_ids, [block for _, block in packed_blocks]))
        packed = in_order(list(zip(offsets, packed_values)), 'x', n_tp)

        def gather_q(values):
            whole = lax.all_gather(values.reshape(-1, width), ('z', 'y'), axis=0, tiled=True)
            return whole.reshape(n_q, n_tp, -1, width)

        def weight(gathered, lo, hi):
            return rounded(jnp.swapaxes(gathered[:, :, lo:hi], 0, 1).reshape(-1, width))

        attn_all, ffn_all = gather_q(packed[:, :starts[2]]), gather_q(packed[:, starts[2]:])
        wt_qkv = weight(attn_all, starts[0], starts[1])
        wf_out = weight(attn_all, starts[1], starts[2])
        bias_all = attn_all[0, :, :starts[0]].reshape(n_tp, -1)
        bf_qkv = bias_all[:, :qkv_cols].reshape(1, -1)
        bf_ffn = bias_all[:, qkv_cols:qkv_cols + 2 * ffn_cols].reshape(1, -1)

        later = emb_table.at[later_ids].get(mode='promise_in_bounds').reshape(n_tp - 1, 2, quarter, width)
        first = first.reshape(2, quarter, width)

        def masked(found, step, way):
            return jnp.where(ring_here[step, way][:, None], found.astype(F32), 0.0)

        top_sum, low_sum = masked(first[0], 0, 0), masked(first[1], 0, 1)
        cos_tab, sin_tab = rope_tables(seq_len, 64)
        order = (xi + jnp.array([0, n_tp - 1, 1, 2], jnp.int32)) % n_tp
        target_ids = jnp.concatenate([line_ids, half_of(line_tokens, 1 - ci, 1)], axis=1)
        target_ids = jnp.where((target_ids >= 0) & (target_ids < vocab_loc), target_ids, -1)
        target_ids = jnp.take(target_ids, order, axis=0).reshape(-1)
        for step in range(1, n_tp):
            top_in, low_in = lax.ppermute(top_sum, 'x', right), lax.ppermute(low_sum, 'x', left)
            if step == 3:
                top_in, low_in, wt_qkv, wf_out, bf_qkv, bf_ffn, cos_tab, sin_tab = lax.optimization_barrier(
                    (top_in, low_in, wt_qkv, wf_out, bf_qkv, bf_ffn, cos_tab, sin_tab))
            top_sum = top_in + masked(later[step - 1, 0], step, 0)
            low_sum = low_in + masked(later[step - 1, 1], step, 1)
        e_own = jnp.concatenate([top_sum, low_sum], axis=0)

        down_own = half_of(w_down, ci, 0).astype(F32)
        e_own, down_own = lax.optimization_barrier((e_own, down_own))
        down_left, down_right = lax.ppermute(down_own, 'x', right), lax.ppermute(down_own, 'x', left)

        g_seq = lax.dynamic_slice_in_dim(cotangent, xi % seqs, 1, 0)[0]
        g_other = swap(half_of(g_seq, 1 - ci, 0).astype(F32))
        g_own = jnp.where(xi // seqs == ci, half_of(g_seq, ci, 0).astype(F32), g_other)

        core = ci.astype(jnp.int32).reshape(1)
        blk = min(256, half)

        def both_halves(own):
            wide = own.astype(F32)
            return jnp.concatenate([own, rounded(swap(wide))], axis=0)

        def sum_halves(left, right_of):
            other = swap(right_of(left[half:]))
            return lax.optimization_barrier(right_of(left[:half])) + other

        emb = both_halves(e_own.astype(BF16))
        qkv = (dot_nt(emb, wt_qkv) + bf_qkv).astype(BF16)
        context = attention_forward(core, qkv, cos_tab, sin_tab, blk)
        context, down_left, down_right = lax.optimization_barrier((context, down_left, down_right))
        mid = ffn_cols // 2
        down_top, down_low = lax.ppermute(down_left[:mid], 'x', right), lax.ppermute(down_right[mid:], 'x', left)
        near = in_order([(0, rounded(down_own)), (-1, rounded(down_left)), (1, rounded(down_right))], 'x', n_tp)
        attn_out = sum_halves(context, lambda rows: dot(rows, wf_out)) + b_out.astype(F32)
        normed_one, norm_one_pull = jax.vjp(norm_scaled, ALPHA * e_own + attn_out, ln1_gain.astype(F32))
        z_own = (normed_one + ln1_bias.astype(F32)).astype(BF16)
        hidden = both_halves(z_own)
        inner_act, act, slope, wt_ffn = geglu_forward(hidden, ffn_all, bf_ffn, n_tp)
        inner_act, down_top, down_low = lax.optimization_barrier((inner_act, down_top, down_low))
        wf_down = lax.dynamic_update_index_in_dim(near, rounded(jnp.concatenate([down_top, down_low], axis=0)), (xi + 2) % n_tp, 0).reshape(-1, width)
        ffn_out = sum_halves(inner_act, lambda rows: dot(rows, wf_down)) + b_down.astype(F32)
        norm_two_pull = jax.vjp(norm_scaled, ALPHA * z_own.astype(F32) + ffn_out, ln2_gain.astype(F32))[1]

        d_resid_two, d_ln2_gain = norm_two_pull(g_own)
        d_b_down = jnp.sum(d_resid_two, axis=0)
        d_ffn = both_halves(d_resid_two.astype(BF16))

        def scatter_rows(values):
            return lax.psum_scatter(values, ('z', 'y'), scatter_dimension=1, tiled=True)

        def by_shard(values):
            return values.reshape(n_tp, -1, width)

        d_w_down = dot_tn(inner_act, d_ffn)
        down_piece = scatter_rows(by_shard(d_w_down))
        d_pre, d_b_ffn = geglu_backward(d_ffn, wf_down, act, slope, n_tp)
        d_w_ffn = dot_tn(d_pre, hidden)
        ffn_piece = scatter_rows(by_shard(d_w_ffn))
        d_hidden_sum = sum_halves(d_pre, lambda rows: dot(rows, wt_ffn))
        d_hidden = ALPHA * d_resid_two + d_hidden_sum
        d_ln1_bias = jnp.sum(d_hidden, axis=0)
        d_resid_one, d_ln1_gain = norm_one_pull(d_hidden)
        d_b_out = jnp.sum(d_resid_one, axis=0)
        d_attn = both_halves(d_resid_one.astype(BF16))
        d_context = dot_nt(d_attn, wf_out).astype(BF16)
        d_qkv, d_b_qkv = attention_backward(core, qkv, d_context, cos_tab, sin_tab, blk)

        def column_part(which):
            cols = width // 2
            product = dot(d_qkv, lax.dynamic_slice_in_dim(wt_qkv, which * cols, cols, 1))
            direct = ALPHA * lax.dynamic_slice_in_dim(d_resid_one, which * cols, cols, 1)
            return product + jnp.concatenate([direct, jnp.zeros_like(direct)], axis=0)

        sent = column_part(1 - ci)
        other_rows = jnp.concatenate([swap(sent[half:]), swap(sent[:half])], axis=0)
        d_rows = lax.optimization_barrier(column_part(ci)) + other_rows
        from_left, from_right = lax.ppermute(d_rows, 'x', right), lax.ppermute(d_rows, 'x', left)
        d_rows, d_qkv, d_attn = lax.optimization_barrier((d_rows, d_qkv, d_attn))
        d_w_qkv = dot_tn(d_qkv, emb)
        d_w_out = dot_tn(context, d_attn)

        def small_split(values):
            return jnp.pad(values, ((0, 0), (0, -values.shape[1] % (n_q * 8 * width)))).reshape(n_tp, -1, width)

        vec5 = jnp.concatenate([d_b_out, d_ln1_gain, d_ln1_bias, d_b_down, d_ln2_gain])
        small = jnp.concatenate([
            jnp.broadcast_to(vec5, (n_tp, vec5.shape[0])),
            d_b_ffn.reshape(n_tp, -1), d_b_qkv.reshape(n_tp, -1)], axis=1)

        def to_shard(piece):
            total = lax.dynamic_index_in_dim(piece, xi, 0, keepdims=False)
            for step in range(1, n_tp):
                shift = [(i, (i + step) % n_tp) for i in range(n_tp)]
                total = total + lax.ppermute(lax.dynamic_index_in_dim(piece, (xi + step) % n_tp, 0, keepdims=False), 'x', shift)
            return total

        attn = jnp.concatenate([by_shard(d_w_qkv), by_shard(d_w_out), small_split(small)], axis=1)

        attn = scatter_rows(attn)
        far_top = lax.ppermute(from_left[:half], 'x', right)
        far_low = lax.ppermute(from_right[half:], 'x', left)
        row_lists, row_counts = bucket_ids(target_ids, n_tp, vocab_loc)
        d_table = add_rows(row_lists, row_counts, [d_rows, from_left, from_right, far_top, far_low], vocab_loc)
        down_piece, ffn_piece, attn, d_table = lax.optimization_barrier((down_piece, ffn_piece, attn, d_table))
        d_table = lax.psum(d_table, ('z', 'y'))
        down_piece, gate_lin_piece, attn_piece = [to_shard(piece) for piece in (down_piece, ffn_piece, attn)]

        def gather_rows(values, order):
            sizes = {'z': n_z, 'y': n_y}
            for depth, axis in enumerate(order):
                values = in_order(ring_blocks(values, axis, sizes[axis], split=depth == 1), axis, sizes[axis])
            if order == 'zy':
                values = jnp.swapaxes(values, 0, 1)
            values = values.reshape(n_q, -1, width)
            return in_order([(0, values), (1, swap(values))], 'c', 2)

        mixed = gather_rows(jnp.concatenate([down_piece, attn_piece], axis=0), 'yz')
        n_down = down_piece.shape[0]
        d_w_down = mixed[:, :, :n_down].reshape(-1, width)
        gate_lin = gather_rows(gate_lin_piece, 'zy').reshape(2, -1, width)
        d_w_gate = gate_lin[:, :ffn_cols].reshape(-1, width).T
        d_w_lin = gate_lin[:, ffn_cols:].reshape(-1, width).T
        attn = mixed[:, :, n_down:].reshape(2, -1, width)
        out_rows = w_out.shape[0] // 2
        d_w_qkv = jnp.concatenate([head_order(attn[i, :qkv_cols], pairs_loc) for i in (0, 1)], axis=0).T
        d_w_out = attn[:, qkv_cols:qkv_cols + out_rows].reshape(-1, width)
        small = attn[:, qkv_cols + out_rows:].reshape(2, -1)
        d_b_out, d_ln1_gain, d_ln1_bias, d_b_down, d_ln2_gain = [
            small[0, i * width:(i + 1) * width] + small[1, i * width:(i + 1) * width] for i in range(5)]
        at = 5 * width
        d_b_gate = small[:, at:at + ffn_cols].reshape(-1)
        d_b_lin = small[:, at + ffn_cols:at + 2 * ffn_cols].reshape(-1)
        at += 2 * ffn_cols
        d_b_qkv = jnp.concatenate([head_order(small[i, at:at + qkv_cols], pairs_loc) for i in (0, 1)]).reshape(heads_loc, -1)
        d_table, d_w_qkv, d_w_out, d_w_gate, d_w_lin, d_w_down = lax.optimization_barrier((d_table, d_w_qkv, d_w_out, d_w_gate, d_w_lin, d_w_down))
        cols = width // 2
        base = lax.optimization_barrier(jnp.zeros((vocab_loc, width), F32))
        other_table = swap(d_table)
        d_table = lax.dynamic_update_slice_in_dim(base, SHRINK * d_table, ci * cols, 1)
        d_table = lax.dynamic_update_slice_in_dim(d_table, SHRINK * other_table, (1 - ci) * cols, 1)
        return (d_table, d_w_qkv, d_b_qkv, d_w_out, d_b_out, d_ln1_gain, d_ln1_bias, d_w_gate, d_b_gate, d_w_lin, d_b_lin, d_w_down, d_b_down, d_ln2_gain)

    return jax.shard_map(device_step, mesh=fine, in_specs=in_specs, out_specs=out_specs, check_vma=False)
```

profile of v0, /device:TPU:1, one launch (start us, length us, event | category | flops | bytes accessed | tf_op | source)
XLA Modules:
  0.0 1122.3 jit_solution(6815256811974847644)
XLA Ops:
  26.9 15.5 %gather_fusion = bf16[768,1024]{1,0:T(8,128)(2,1)S(1)} fusion(bf16[12576,1024]{1,0:T(8,128)(2,1)} %param.23, s32[1024]{0:T(1024)S(1)} %pad_clamp_fusion.2), kind=kCustom, calls=%fused_computation.4 | custom fusion | bytes 3148800 | tf_op jit(solution)/shard_map/gather | solution.py:469
  53.9 23.3 %gather_fusion.1 = bf16[2304,1024]{1,0:T(8,128)(2,1)} fusion(bf16[12576,1024]{1,0:T(8,128)(2,1)} %param.23, s32[3072]{0:T(1024)S(1)} %pad_clamp_fusion), kind=kCustom, calls=%fused_computation.5 | custom fusion | bytes 9446400 | tf_op jit(solution)/shard_map/gather | solution.py:488
  77.2 10.9 collective-permute-done.7
  89.9 4.0 fusion.15
  99.6 29.0 %collective-permute-done.8 = f32[384,1024]{1,0:T(8,128)S(1)} collective-permute-done((f32[384,1024]{1,0:T(8,128)}, f32[384,1024]{1,0:T(8,128)S(1)}, u32[]{:S(2)}, u32[]{:S(2)}) %collective-permute-start.8) | collective-permute-done | bytes 1572896 | tf_op jit(solution)/shard_map/ppermute | solution.py:501
  130.2 4.1 fusion.14
  142.8 5.9 fusion
  148.7 20.9 %collective-permute-done.6 = f32[384,1024]{1,0:T(8,128)} collective-permute-done((f32[384,1024]{1,0:T(8,128)}, f32[384,1024]{1,0:T(8,128)}, u32[]{:S(2)}, u32[]{:S(2)}) %collective-permute-start.6) | collective-permute-done | bytes 1572896 | tf_op jit(solution)/shard_map/ppermute | solution.py:501
  187.8 7.0 add_convert_fusion.qkv_ref
  194.8 33.4 %attn_fwd.1 = bf16[1536,512]{1,0:T(8,128)(2,1)S(1)} custom-call(s32[1]{0:T(128)} %bitcast.26.core_ref, bf16[1536,1536]{1,0:T(8,128)(2,1)} %add_convert_fusion.qkv_ref, f32[1536,128]{1,0:T(8,128)S(1)} %get-tuple-element.72.cos_ref, f32[1536,128]{1,0:T(8,128)S(1)} %get-tuple-element.73.sin_ref), custom_call_target="tpu_custom_call" | custom-call | flops 4831838208 | bytes 7077888 | tf_op jit(solution)/shard_map/attn_fwd/pallas_call | solution.py:162
  231.8 4.2 collective-permute-done.13
  260.1 25.8 %geglu_fwd.1 = (bf16[1536,2048]{1,0:T(8,128)(2,1)}, f32[1536,2048]{1,0:T(8,128)}, f32[1536,2048]{1,0:T(8,128)}, bf16[4096,1024]{1,0:T(8,128)(2,1)}) custom-call(bf16[1536,1024]{1,0:T(8,128)(2,1)} %pad_maximum_fusion.3.hidden_ref, f32[16,4,64,1024]{3,2,1,0:T(8,128)} %bitcast.310, f32[1,4096]{1,0:T(1,128)} %bitcast.299), custom_call_target="tpu_custom_call" | custom-call | flops 12884901888 | bytes 31457280 | tf_op jit(solution)/shard_map/geglu_fwd/pallas_call | solution.py:219
  288.6 8.2 fusion.5
  301.4 6.3 fusion.7
  319.9 5.7 collective-permute-done.19
  327.9 19.3 %geglu_bwd.1 = (bf16[1536,4096]{1,0:T(8,128)(2,1)}, f32[1,4096]{1,0:T(1,128)}) custom-call(bf16[1536,1024]{1,0:T(8,128)(2,1)} %pad_maximum_fusion.4.d_ffn_ref, bf16[2048,1024]{1,0:T(8,128)(2,1)} %bitcast.36.weight_ref, f32[1536,2048]{1,0:T(8,128)} %get-tuple-element.84.act_ref, f32[1536,2048]{1,0:T(8,128)} %get-tuple-element.85.slope_ref), custom_call_target="tpu_custom_call" | custom-call | flops 6442450944 | bytes 37748736 | tf_op jit(solution)/shard_map/geglu_bwd/pallas_call | solution.py:250
  347.2 12.0 %fusion.1 = f32[768,1024]{1,0:T(8,128)} fusion(bf16[4096,1024]{1,0:T(8,128)(2,1)} %get-tuple-element.87, bf16[1536,4096]{1,0:T(8,128)(2,1)} %get-tuple-element.86), kind=kOutput, calls=%fused_computation.13 | convolution fusion | flops 6442450944 | bytes 17825792 | tf_op jit(solution)/shard_map/dot_general | solution.py:40
  359.8 10.8 fusion.59
  370.7 11.0 fusion.3
  400.7 58.3 %attn_bwd.1 = (bf16[1536,1536]{1,0:T(8,128)(2,1)}, f32[1,1536]{1,0:T(1,128)}) custom-call(s32[1]{0:T(128)} %bitcast.26.core_ref, bf16[1536,1536]{1,0:T(8,128)(2,1)} %add_convert_fusion.qkv_ref, bf16[1536,512]{1,0:T(8,128)(2,1)} %convolution_convert_fusion.dctx_ref, f32[1536,128]{1,0:T(8,128)} %copy-done.6, f32[1536,128]{1,0:T(8,128)} %copy-done.7), custom_call_target="tpu_custom_call" | custom-call | flops 12079595520 | bytes 11796480 | tf_op jit(solution)/shard_map/attn_bwd/pallas_call | solution.py:182
  459.8 6.0 convolution_add_fusion
  475.9 5.2 fusion.11
  481.1 4.8 pad_maximum_fusion
  486.2 20.5 %fusion.60 = f32[4096,1024]{1,0:T(8,128)} fusion(bf16[1536,4096]{1,0:T(8,128)(2,1)} %get-tuple-element.86, bf16[768,1024]{1,0:T(8,128)(2,1)} %copy-done.19, bf16[768,1024]{1,0:T(8,128)(2,1)} %copy-done.14), kind=kOutput, calls=%fused_computation.259 | convolution fusion | flops 12891193344 | bytes 32505856 | tf_op jit(solution)/shard_map/dot_general | solution.py:44
  509.6 67.6 %collective-permute-done.24.refs_1_ = f32[1536,512]{1,0:T(8,128)S(1)} collective-permute-done((f32[1536,512]{1,0:T(8,128)S(1)}, f32[1536,512]{1,0:T(8,128)S(1)}, u32[]{:S(2)}, u32[]{:S(2)}) %collective-permute-start.24) | collective-permute-done | bytes 3145760 | tf_op jit(solution)/shard_map/ppermute | solution.py:578
  584.1 31.5 %bucket_ids.1 = (s32[30720]{0:T(1024)}, s32[20]{0:T(128)}) custom-call(s32[6144]{0:T(1024)} %get-tuple-element.210.group_ref, s32[6144]{0:T(1024)} %get-tuple-element.209.value_ref), custom_call_target="tpu_custom_call" | custom-call | flops 40000000 | bytes 122880 | tf_op jit(solution)/shard_map/bucket_ids/pallas_call | solution.py:288
  619.2 39.6 %table_rows.1 = f32[12576,512]{1,0:T(8,128)} custom-call(s32[30720]{0:T(1024)S(1)} %copy-done.8, s32[20]{0:T(128)S(1)} %copy-done.9, f32[1536,512]{1,0:T(8,128)S(1)} %maximum_add_fusion.refs_0_, f32[1536,512]{1,0:T(8,128)S(1)} %copy-done.3, f32[1536,512]{1,0:T(8,128)} %copy-done.18, f32[768,512]{1,0:T(8,128)} %collective-permute-done.26.refs_3_, ...), custom_call_target="tpu_custom_call" | custom-call | flops 193167360 | bytes 25755648 | tf_op jit(solution)/shard_map/table_rows/pallas_call | solution.py:356
  658.9 31.5 %reduce-scatter.6.cloned.1.call-done = f32[4,64,1024]{2,1,0:T(8,128)} async-done(((f32[4,1024,1024]{2,1,0:T(8,128)}), f32[4,64,1024]{2,1,0:T(8,128)}) %reduce-scatter.6.cloned.1.call-update) | async-done | bytes 1048592 | tf_op jit(solution)/shard_map/reduce_scatter | solution.py:550
  697.1 6.1 collective-permute-done.30
  703.4 5.4 collective-permute-start.44
  718.7 5.0 collective-permute-done.42
  730.6 4.3 collective-permute-done.45
  735.3 12.4 %collective-permute-done.47 = f32[64,1024]{1,0:T(8,128)S(1)} collective-permute-done((f32[64,1024]{1,0:T(8,128)S(1)}, f32[64,1024]{1,0:T(8,128)S(1)}, u32[]{:S(2)}, u32[]{:S(2)}) %collective-permute-start.47) | collective-permute-done | bytes 262176 | tf_op jit(solution)/shard_map/ppermute | solution.py:384
  759.5 35.9 %collective-permute-done.49 = f32[4,64,1024]{2,1,0:T(8,128)S(1)} collective-permute-done((f32[4,64,1024]{2,1,0:T(8,128)S(1)}, f32[4,64,1024]{2,1,0:T(8,128)S(1)}, u32[]{:S(2)}, u32[]{:S(2)}) %collective-permute-start.49) | collective-permute-done | bytes 1048608 | tf_op jit(solution)/shard_map/ppermute | solution.py:379
  804.5 15.5 %collective-permute-done.51 = f32[2,64,1024]{2,1,0:T(8,128)S(1)} collective-permute-done((f32[2,64,1024]{2,1,0:T(8,128)S(1)}, f32[2,64,1024]{2,1,0:T(8,128)S(1)}, u32[]{:S(2)}, u32[]{:S(2)}) %collective-permute-start.51) | collective-permute-done | bytes 524320 | tf_op jit(solution)/shard_map/ppermute | solution.py:382
  824.6 5.1 collective-permute-start.52
  833.2 6.6 collective-permute-start.41
  843.7 4.8 broadcast_in_dim.296
  848.5 5.2 bitcast_dynamic-update-slice_fusion.1
  856.5 4.2 fusion.71
  860.8 5.4 copy.72
  866.2 5.4 copy.73
  871.6 5.2 bitcast_dynamic-update-slice_fusion
  880.1 4.8 slice.331
  888.7 166.6 %all-reduce.6.cloned.1.call-done = f32[12576,512]{1,0:T(8,128)} async-done(((f32[12576,512]{1,0:T(8,128)}), f32[12576,512]{1,0:T(8,128)}) %all-reduce.6.cloned.1.call-update) | async-done | bytes 25755664 | tf_op jit(solution)/shard_map/psum | solution.py:606
  1063.4 24.3 %broadcast_in_dim.258 = f32[12576,1024]{1,0:T(8,128)} broadcast(f32[]{:T(128)} %constant.441.clone.1), dimensions={} | broadcast | bytes 51511300 | tf_op jit(solution)/shard_map/broadcast_in_dim | solution.py:638
  1087.7 9.2 multiply_dynamic-update-slice_fusion.1
  1096.9 18.1 %multiply_dynamic-update-slice_fusion = f32[12576,1024]{1,0:T(8,128)} fusion(f32[12576,1024]{1,0:T(8,128)} %multiply_dynamic-update-slice_fusion.1, s32[]{:T(128)S(6)} %select_n.428, f32[12576,512]{1,0:T(8,128)} %collective-permute-done.53), kind=kLoop, calls=%fused_computation.7 | loop fusion | flops 6438912 | bytes 51511300 | tf_op jit(solution)/shard_map/dynamic_update_slice | solution.py:641
  (429 shorter events, 234.0 us)
Async XLA Ops:
  7.2 131.8 %all-gather.3.cloned.1.call-start = ((), (), s32[]{:S(2)}) async-start(), calls=%async_computation.3 | async-start | bytes 11141120 | tf_op jit(solution)/shard_map/all_gather | solution.py:475
  17.4 25.0 %collective-permute-start.1 = (f32[104,1024]{1,0:T(8,128)S(1)}, f32[104,1024]{1,0:T(8,128)S(1)}, u32[]{:S(2)}, u32[]{:S(2)}) collective-permute-start(f32[104,1024]{1,0:T(8,128)S(1)} %pad_maximum_fusion.10), channel_id=1, source_target_pairs={{0,32},{32,64},{64,96},{96,0},{1,33},{33,65},{65,97},{97,1},{2,34}... | collective-permute-start | bytes 1277960 | tf_op jit(solution)/shard_map/ppermute | solution.py:379
  19.5 22.9 %collective-permute-start.2 = (f32[104,1024]{1,0:T(8,128)S(1)}, f32[104,1024]{1,0:T(8,128)S(1)}, u32[]{:S(2)}, u32[]{:S(2)}) collective-permute-start(f32[104,1024]{1,0:T(8,128)S(1)} %pad_maximum_fusion.10), channel_id=1, source_target_pairs={{0,96},{32,0},{64,32},{96,64},{1,97},{33,1},{65,33},{97,65},{2,98}... | collective-permute-start | bytes 1277960 | tf_op jit(solution)/shard_map/ppermute | solution.py:379
  20.8 23.1 %collective-permute-start.3 = (f32[104,1024]{1,0:T(8,128)S(1)}, f32[104,1024]{1,0:T(8,128)}, u32[]{:S(2)}, u32[]{:S(2)}) collective-permute-start(f32[104,1024]{1,0:T(8,128)S(1)} %pad_maximum_fusion.10), channel_id=1, source_target_pairs={{0,64},{32,96},{64,0},{96,32},{1,65},{33,97},{65,1},{97,33},{2,66}... | collective-permute-start | bytes 1277960 | tf_op jit(solution)/shard_map/ppermute | solution.py:384
  48.2 211.8 %all-gather.5.cloned.1.call-start = ((), (), s32[]{:S(2)}) async-start(), calls=%async_computation.4 | async-start | bytes 17825792 | tf_op jit(solution)/shard_map/all_gather | solution.py:475
  49.4 609.5 %reduce-scatter.4.cloned.1.call-start = ((), (), s32[]{:S(2)}) async-start(), calls=%async_computation.5 | async-start | bytes 8912896 | tf_op jit(solution)/shard_map/reduce_scatter | solution.py:550
  52.2 35.9 %collective-permute-start.7 = (f32[384,1024]{1,0:T(8,128)}, f32[384,1024]{1,0:T(8,128)S(1)}, u32[]{:S(2)}, u32[]{:S(2)}) collective-permute-start(f32[384,1024]{1,0:T(8,128)} %get-tuple-element.191), channel_id=1, source_target_pairs={{0,96},{32,0},{64,32},{96,64},{1,97},{33,1},{65,33},{97,65},{2,98}... | collective-permute-start | bytes 4718600 | tf_op jit(solution)/shard_map/ppermute | solution.py:501
  53.0 36.8 %collective-permute-start.4 = (f32[384,1024]{1,0:T(8,128)S(1)}, f32[384,1024]{1,0:T(8,128)}, u32[]{:S(2)}, u32[]{:S(2)}) collective-permute-start(f32[384,1024]{1,0:T(8,128)S(1)} %get-tuple-element.192), channel_id=1, source_target_pairs={{0,32},{32,64},{64,96},{96,0},{1,33},{33,65},{65,97},{97,1},{2,34}... | collective-permute-start | bytes 4718600 | tf_op jit(solution)/shard_map/ppermute | solution.py:501
  93.8 34.7 %collective-permute-start.8 = (f32[384,1024]{1,0:T(8,128)}, f32[384,1024]{1,0:T(8,128)S(1)}, u32[]{:S(2)}, u32[]{:S(2)}) collective-permute-start(f32[384,1024]{1,0:T(8,128)} %get-tuple-element.184), channel_id=1, source_target_pairs={{0,96},{32,0},{64,32},{96,64},{1,97},{33,1},{65,33},{97,65},{2,98}... | collective-permute-start | bytes 4718600 | tf_op jit(solution)/shard_map/ppermute | solution.py:501
  94.1 36.1 %collective-permute-start.5 = (f32[384,1024]{1,0:T(8,128)}, f32[384,1024]{1,0:T(8,128)}, u32[]{:S(2)}, u32[]{:S(2)}) collective-permute-start(f32[384,1024]{1,0:T(8,128)} %get-tuple-element.185), channel_id=1, source_target_pairs={{0,32},{32,64},{64,96},{96,0},{1,33},{33,65},{65,97},{97,1},{2,34}... | collective-permute-start | bytes 4718600 | tf_op jit(solution)/shard_map/ppermute | solution.py:501
  134.3 35.2 %collective-permute-start.6 = (f32[384,1024]{1,0:T(8,128)}, f32[384,1024]{1,0:T(8,128)}, u32[]{:S(2)}, u32[]{:S(2)}) collective-permute-start(f32[384,1024]{1,0:T(8,128)} %get-tuple-element.183), channel_id=1, source_target_pairs={{0,32},{32,64},{64,96},{96,0},{1,33},{33,65},{65,97},{97,1},{2,34}... | collective-permute-start | bytes 4718600 | tf_op jit(solution)/shard_map/ppermute | solution.py:501
  134.3 35.2 %collective-permute-start.9 = (f32[384,1024]{1,0:T(8,128)}, f32[384,1024]{1,0:T(8,128)}, u32[]{:S(2)}, u32[]{:S(2)}) collective-permute-start(f32[384,1024]{1,0:T(8,128)} %get-tuple-element.182), channel_id=1, source_target_pairs={{0,96},{32,0},{64,32},{96,64},{1,97},{33,1},{65,33},{97,65},{2,98}... | collective-permute-start | bytes 4718600 | tf_op jit(solution)/shard_map/ppermute | solution.py:501
  179.8 49.0 %collective-permute-start.11 = (f32[512,1024]{1,0:T(8,128)}, f32[512,1024]{1,0:T(8,128)}, u32[]{:S(2)}, u32[]{:S(2)}) collective-permute-start(f32[512,1024]{1,0:T(8,128)} %dynamic-slice_convert_fusion), channel_id=1, source_target_pairs={{0,32},{32,64},{64,96},{96,0},{1,33},{33,65},{65,97},{97,1},{2,34}... | collective-permute-start | bytes 6291464 | tf_op jit(solution)/shard_map/ppermute | solution.py:511
  179.8 49.0 %collective-permute-start.12 = (f32[512,1024]{1,0:T(8,128)}, f32[512,1024]{1,0:T(8,128)}, u32[]{:S(2)}, u32[]{:S(2)}) collective-permute-start(f32[512,1024]{1,0:T(8,128)} %dynamic-slice_convert_fusion), channel_id=1, source_target_pairs={{0,96},{32,0},{64,32},{96,64},{1,97},{33,1},{65,33},{97,65},{2,98}... | collective-permute-start | bytes 6291464 | tf_op jit(solution)/shard_map/ppermute | solution.py:511
  237.7 18.7 %collective-permute-start.14 = (f32[768,1024]{1,0:T(8,128)S(1)}, f32[768,1024]{1,0:T(8,128)S(1)}, u32[]{:S(2)}, u32[]{:S(2)}) collective-permute-start(f32[768,1024]{1,0:T(8,128)S(1)} %get-tuple-element.166), channel_id=1, source_target_pairs={{0,1},{1,0},{2,3},{3,2},{4,5},{5,4},{6,7},{7,6},{8,9},{9,8},{10,11... | collective-permute-start | bytes 9437192 | tf_op jit(solution)/shard_map/ppermute | solution.py:21
  245.9 39.9 %collective-permute-start.15 = (f32[256,1024]{1,0:T(8,128)}, f32[256,1024]{1,0:T(8,128)}, u32[]{:S(2)}, u32[]{:S(2)}) collective-permute-start(f32[256,1024]{1,0:T(8,128)} %slice.242), channel_id=1, source_target_pairs={{0,32},{32,64},{64,96},{96,0},{1,33},{33,65},{65,97},{97,1},{2,34}... | collective-permute-start | bytes 3145736 | tf_op jit(solution)/shard_map/ppermute | solution.py:533
  249.1 36.7 %collective-permute-start.16 = (f32[256,1024]{1,0:T(8,128)}, f32[256,1024]{1,0:T(8,128)}, u32[]{:S(2)}, u32[]{:S(2)}) collective-permute-start(f32[256,1024]{1,0:T(8,128)} %slice.243), channel_id=1, source_target_pairs={{0,96},{32,0},{64,32},{96,64},{1,97},{33,1},{65,33},{97,65},{2,98}... | collective-permute-start | bytes 3145736 | tf_op jit(solution)/shard_map/ppermute | solution.py:533
  296.8 10.8 collective-permute-start.18
  359.3 22.5 %collective-permute-start.20 = (f32[768,1024]{1,0:T(8,128)}, f32[768,1024]{1,0:T(8,128)}, u32[]{:S(2)}, u32[]{:S(2)}) collective-permute-start(f32[768,1024]{1,0:T(8,128)} %fusion.1), channel_id=1, source_target_pairs={{0,1},{1,0},{2,3},{3,2},{4,5},{5,4},{6,7},{7,6},{8,9},{9,8},{10,11... | collective-permute-start | bytes 9437192 | tf_op jit(solution)/shard_map/ppermute | solution.py:21
  370.6 288.2 %reduce-scatter.8.cloned.1.call-start = ((), (), s32[]{:S(2)}) async-start(), calls=%async_computation.7 | async-start | bytes 11141120 | tf_op jit(solution)/shard_map/reduce_scatter | solution.py:550
  485.9 204.4 %reduce-scatter.6.cloned.1.call-start = ((), (), s32[]{:S(2)}) async-start(), calls=%async_computation.6 | async-start | bytes 17825792 | tf_op jit(solution)/shard_map/reduce_scatter | solution.py:550
  506.7 548.5 %all-reduce.6.cloned.1.call-start = ((), (), s32[]{:S(2)}) async-start(), calls=%async_computation.8 | async-start | bytes 51511296 | tf_op jit(solution)/shard_map/psum | solution.py:606
  506.8 70.4 %collective-permute-start.24 = (f32[1536,512]{1,0:T(8,128)S(1)}, f32[1536,512]{1,0:T(8,128)S(1)}, u32[]{:S(2)}, u32[]{:S(2)}) collective-permute-start(f32[1536,512]{1,0:T(8,128)S(1)} %maximum_add_fusion.refs_0_), channel_id=1, source_target_pairs={{0,32},{32,64},{64,96},{96,0},{1,33},{33,65},{65,97},{97,1},{2,34}... | collective-permute-start | bytes 9437192 | tf_op jit(solution)/shard_map/ppermute | solution.py:578
  507.0 71.5 %collective-permute-start.25 = (f32[1536,512]{1,0:T(8,128)S(1)}, f32[1536,512]{1,0:T(8,128)S(1)}, u32[]{:S(2)}, u32[]{:S(2)}) collective-permute-start(f32[1536,512]{1,0:T(8,128)S(1)} %maximum_add_fusion.refs_0_), channel_id=1, source_target_pairs={{0,96},{32,0},{64,32},{96,64},{1,97},{33,1},{65,33},{97,65},{2,98}... | collective-permute-start | bytes 9437192 | tf_op jit(solution)/shard_map/ppermute | solution.py:578
  578.5 37.1 %collective-permute-start.26 = (f32[768,512]{1,0:T(8,128)}, f32[768,512]{1,0:T(8,128)}, u32[]{:S(2)}, u32[]{:S(2)}) collective-permute-start(f32[768,512]{1,0:T(8,128)} %slice.319), channel_id=1, source_target_pairs={{0,32},{32,64},{64,96},{96,0},{1,33},{33,65},{65,97},{97,1},{2,34}... | collective-permute-start | bytes 4718600 | tf_op jit(solution)/shard_map/ppermute | solution.py:601
  580.0 35.6 %collective-permute-start.27 = (f32[768,512]{1,0:T(8,128)}, f32[768,512]{1,0:T(8,128)}, u32[]{:S(2)}, u32[]{:S(2)}) collective-permute-start(f32[768,512]{1,0:T(8,128)} %slice.320), channel_id=1, source_target_pairs={{0,96},{32,0},{64,32},{96,64},{1,97},{33,1},{65,33},{97,65},{2,98}... | collective-permute-start | bytes 4718600 | tf_op jit(solution)/shard_map/ppermute | solution.py:602
  690.6 19.5 %collective-permute-start.33 = (f32[40,1024]{1,0:T(8,128)S(1)}, f32[40,1024]{1,0:T(8,128)S(1)}, u32[]{:S(2)}, u32[]{:S(2)}) collective-permute-start(f32[40,1024]{1,0:T(8,128)S(1)} %get-tuple-element.204), channel_id=1, source_target_pairs={{0,96},{32,0},{64,32},{96,64},{1,97},{33,1},{65,33},{97,65},{2,98}... | collective-permute-start | bytes 491528 | tf_op jit(solution)/shard_map/ppermute | solution.py:595
  693.1 17.8 %collective-permute-start.32 = (f32[40,1024]{1,0:T(8,128)S(1)}, f32[40,1024]{1,0:T(8,128)S(1)}, u32[]{:S(2)}, u32[]{:S(2)}) collective-permute-start(f32[40,1024]{1,0:T(8,128)S(1)} %get-tuple-element.205), channel_id=1, source_target_pairs={{0,64},{32,96},{64,0},{96,32},{1,65},{33,97},{65,1},{97,33},{2,66}... | collective-permute-start | bytes 491528 | tf_op jit(solution)/shard_map/ppermute | solution.py:595
  696.3 12.6 %collective-permute-start.28 = (f32[32,1024]{1,0:T(8,128)S(1)}, f32[32,1024]{1,0:T(8,128)S(1)}, u32[]{:S(2)}, u32[]{:S(2)}) collective-permute-start(f32[32,1024]{1,0:T(8,128)S(1)} %get-tuple-element.206), channel_id=1, source_target_pairs={{0,32},{32,64},{64,96},{96,0},{1,33},{33,65},{65,97},{97,1},{2,34}... | collective-permute-start | bytes 393224 | tf_op jit(solution)/shard_map/ppermute | solution.py:595
  703.4 15.2 %collective-permute-start.44 = (f32[64,1024]{1,0:T(8,128)S(1)}, f32[64,1024]{1,0:T(8,128)S(1)}, u32[]{:S(2)}, u32[]{:S(2)}) collective-permute-start(f32[64,1024]{1,0:T(8,128)S(1)} %get-tuple-element.201), channel_id=1, source_target_pairs={{0,96},{32,0},{64,32},{96,64},{1,97},{33,1},{65,33},{97,65},{2,98}... | collective-permute-start | bytes 786440 | tf_op jit(solution)/shard_map/ppermute | solution.py:595
  710.1 13.5 %collective-permute-start.42 = (f32[64,1024]{1,0:T(8,128)S(1)}, f32[64,1024]{1,0:T(8,128)S(1)}, u32[]{:S(2)}, u32[]{:S(2)}) collective-permute-start(f32[64,1024]{1,0:T(8,128)S(1)} %get-tuple-element.200), channel_id=1, source_target_pairs={{0,32},{32,64},{64,96},{96,0},{1,33},{33,65},{65,97},{97,1},{2,34}... | collective-permute-start | bytes 786440 | tf_op jit(solution)/shard_map/ppermute | solution.py:595
  712.0 15.9 %collective-permute-start.34 = (f32[72,1024]{1,0:T(8,128)S(1)}, f32[72,1024]{1,0:T(8,128)S(1)}, u32[]{:S(2)}, u32[]{:S(2)}) collective-permute-start(f32[72,1024]{1,0:T(8,128)S(1)} %pad_maximum_fusion.11), channel_id=1, source_target_pairs={{0,2},{2,4},{4,6},{6,0},{1,3},{3,5},{5,7},{7,1},{8,10},{10,12},{12... | collective-permute-start | bytes 884744 | tf_op jit(solution)/shard_map/ppermute | solution.py:379
  713.1 37.4 %collective-permute-start.35 = (f32[72,1024]{1,0:T(8,128)S(1)}, f32[72,1024]{1,0:T(8,128)S(1)}, u32[]{:S(2)}, u32[]{:S(2)}) collective-permute-start(f32[72,1024]{1,0:T(8,128)S(1)} %pad_maximum_fusion.11), channel_id=1, source_target_pairs={{0,6},{2,0},{4,2},{6,4},{1,7},{3,1},{5,3},{7,5},{8,14},{10,8},{12,... | collective-permute-start | bytes 884744 | tf_op jit(solution)/shard_map/ppermute | solution.py:379
  718.7 31.9 %collective-permute-start.36 = (f32[72,1024]{1,0:T(8,128)S(1)}, f32[72,1024]{1,0:T(8,128)S(1)}, u32[]{:S(2)}, u32[]{:S(2)}) collective-permute-start(f32[72,1024]{1,0:T(8,128)S(1)} %pad_maximum_fusion.11), channel_id=1, source_target_pairs={{0,4},{2,6},{4,0},{6,2},{1,5},{3,7},{5,1},{7,3},{8,12},{10,14},{12... | collective-permute-start | bytes 884744 | tf_op jit(solution)/shard_map/ppermute | solution.py:384
  723.8 11.1 collective-permute-start.45
  725.0 10.4 collective-permute-start.46
  728.0 19.8 %collective-permute-start.47 = (f32[64,1024]{1,0:T(8,128)S(1)}, f32[64,1024]{1,0:T(8,128)S(1)}, u32[]{:S(2)}, u32[]{:S(2)}) collective-permute-start(f32[64,1024]{1,0:T(8,128)S(1)} %get-tuple-element.150), channel_id=1, source_target_pairs={{0,16},{8,24},{16,0},{24,8},{1,17},{9,25},{17,1},{25,9},{2,18},{10... | collective-permute-start | bytes 786440 | tf_op jit(solution)/shard_map/ppermute | solution.py:384
  747.8 50.6 %collective-permute-start.48 = (f32[4,64,1024]{2,1,0:T(8,128)S(1)}, f32[4,64,1024]{2,1,0:T(8,128)S(1)}, u32[]{:S(2)}, u32[]{:S(2)}) collective-permute-start(f32[4,64,1024]{2,1,0:T(8,128)S(1)} %bitcast_dynamic-update-slice_fusion.17), channel_id=1, source_target_pairs={{0,2},{2,4},{4,6},{6,0},{1,3},{3,5},{5,7},{7,1},{8,10},{10,12},{12... | collective-permute-start | bytes 3145736 | tf_op jit(solution)/shard_map/ppermute | solution.py:379
  748.9 46.6 %collective-permute-start.49 = (f32[4,64,1024]{2,1,0:T(8,128)S(1)}, f32[4,64,1024]{2,1,0:T(8,128)S(1)}, u32[]{:S(2)}, u32[]{:S(2)}) collective-permute-start(f32[4,64,1024]{2,1,0:T(8,128)S(1)} %bitcast_dynamic-update-slice_fusion.17), channel_id=1, source_target_pairs={{0,6},{2,0},{4,2},{6,4},{1,7},{3,1},{5,3},{7,5},{8,14},{10,8},{12,... | collective-permute-start | bytes 3145736 | tf_op jit(solution)/shard_map/ppermute | solution.py:379
  750.6 52.2 %collective-permute-start.38 = (f32[4,72,1024]{2,1,0:T(8,128)S(1)}, f32[4,72,1024]{2,1,0:T(8,128)S(1)}, u32[]{:S(2)}, u32[]{:S(2)}) collective-permute-start(f32[4,72,1024]{2,1,0:T(8,128)S(1)} %bitcast_dynamic-update-slice_fusion.13), channel_id=1, source_target_pairs={{0,24},{8,0},{16,8},{24,16},{1,25},{9,1},{17,9},{25,17},{2,26},{10... | collective-permute-start | bytes 3538952 | tf_op jit(solution)/shard_map/ppermute | solution.py:379
  751.2 53.1 %collective-permute-start.37 = (f32[4,72,1024]{2,1,0:T(8,128)S(1)}, f32[4,72,1024]{2,1,0:T(8,128)S(1)}, u32[]{:S(2)}, u32[]{:S(2)}) collective-permute-start(f32[4,72,1024]{2,1,0:T(8,128)S(1)} %bitcast_dynamic-update-slice_fusion.13), channel_id=1, source_target_pairs={{0,8},{8,16},{16,24},{24,0},{1,9},{9,17},{17,25},{25,1},{2,10},{10... | collective-permute-start | bytes 3538952 | tf_op jit(solution)/shard_map/ppermute | solution.py:379
  795.5 24.5 %collective-permute-start.51 = (f32[2,64,1024]{2,1,0:T(8,128)S(1)}, f32[2,64,1024]{2,1,0:T(8,128)S(1)}, u32[]{:S(2)}, u32[]{:S(2)}) collective-permute-start(f32[2,64,1024]{2,1,0:T(8,128)S(1)} %slice.328), channel_id=1, source_target_pairs={{0,6},{2,0},{4,2},{6,4},{1,7},{3,1},{5,3},{7,5},{8,14},{10,8},{12,... | collective-permute-start | bytes 1572872 | tf_op jit(solution)/shard_map/ppermute | solution.py:382
  798.4 25.1 %collective-permute-start.50 = (f32[2,64,1024]{2,1,0:T(8,128)S(1)}, f32[2,64,1024]{2,1,0:T(8,128)S(1)}, u32[]{:S(2)}, u32[]{:S(2)}) collective-permute-start(f32[2,64,1024]{2,1,0:T(8,128)S(1)} %slice.327), channel_id=1, source_target_pairs={{0,2},{2,4},{4,6},{6,0},{1,3},{3,5},{5,7},{7,1},{8,10},{10,12},{12... | collective-permute-start | bytes 1572872 | tf_op jit(solution)/shard_map/ppermute | solution.py:382
  802.8 29.1 %collective-permute-start.40 = (f32[2,72,1024]{2,1,0:T(8,128)S(1)}, f32[2,72,1024]{2,1,0:T(8,128)S(1)}, u32[]{:S(2)}, u32[]{:S(2)}) collective-permute-start(f32[2,72,1024]{2,1,0:T(8,128)S(1)} %slice.322), channel_id=1, source_target_pairs={{0,24},{8,0},{16,8},{24,16},{1,25},{9,1},{17,9},{25,17},{2,26},{10... | collective-permute-start | bytes 1769480 | tf_op jit(solution)/shard_map/ppermute | solution.py:382
  804.4 27.7 %collective-permute-start.39 = (f32[2,72,1024]{2,1,0:T(8,128)S(1)}, f32[2,72,1024]{2,1,0:T(8,128)S(1)}, u32[]{:S(2)}, u32[]{:S(2)}) collective-permute-start(f32[2,72,1024]{2,1,0:T(8,128)S(1)} %slice.321), channel_id=1, source_target_pairs={{0,8},{8,16},{16,24},{24,0},{1,9},{9,17},{17,25},{25,1},{2,10},{10... | collective-permute-start | bytes 1769480 | tf_op jit(solution)/shard_map/ppermute | solution.py:382
  824.6 29.1 %collective-permute-start.52 = (f32[16,64,1024]{2,1,0:T(8,128)}, f32[16,64,1024]{2,1,0:T(8,128)}, u32[]{:S(2)}, u32[]{:S(2)}) collective-permute-start(f32[16,64,1024]{2,1,0:T(8,128)} %bitcast.87), channel_id=1, source_target_pairs={{0,1},{1,0},{2,3},{3,2},{4,5},{5,4},{6,7},{7,6},{8,9},{9,8},{10,11... | collective-permute-start | bytes 12582920 | tf_op jit(solution)/shard_map/ppermute | solution.py:21
  833.2 38.5 %collective-permute-start.41 = (f32[16,72,1024]{2,1,0:T(8,128)}, f32[16,72,1024]{2,1,0:T(8,128)}, u32[]{:S(2)}, u32[]{:S(2)}) collective-permute-start(f32[16,72,1024]{2,1,0:T(8,128)} %bitcast.58), channel_id=1, source_target_pairs={{0,1},{1,0},{2,3},{3,2},{4,5},{5,4},{6,7},{7,6},{8,9},{9,8},{10,11... | collective-permute-start | bytes 14155784 | tf_op jit(solution)/shard_map/ppermute | solution.py:21
  1055.3 41.6 %collective-permute-start.53 = (f32[12576,512]{1,0:T(8,128)}, f32[12576,512]{1,0:T(8,128)}, u32[]{:S(2)}, u32[]{:S(2)}) collective-permute-start(f32[12576,512]{1,0:T(8,128)} %all-reduce.6.cloned.1.call-done), channel_id=1, source_target_pairs={{0,1},{1,0},{2,3},{3,2},{4,5},{5,4},{6,7},{7,6},{8,9},{9,8},{10,11... | collective-permute-start | bytes 77266952 | tf_op jit(solution)/shard_map/ppermute | solution.py:21
  (73 other events, 975.5 us)
Sparse Core Ops, SparseCore 0:
  48.3 81.0 all-gather.2
  131.5 110.9 all-gather.4
  370.8 85.1 reduce-scatter.3
  486.1 90.2 reduce-scatter.7
  579.6 110.7 reduce-scatter.5
  694.5 360.7 all-reduce.5
where the time goes:
time: 1130 us; the launch traced here: 1120 us
  waiting for transfers between devices  438 us (39%)
  Pallas kernels  208 us (18%)
  local copies, waits for them, and re-layouts  170 us (15%)
  other arithmetic  118 us (10%)
  matrix products  96.4 us (9%)
  starting transfers between devices  75.5 us (7%)
  between operations  16.4 us (1%)
    psum x1, waiting for transfers between devices, device_step(): d_table = lax.psum(d_table, ('z', 'y'))  167 us
    ppermute x1, waiting for transfers between devices, device_step(): lax.ppermute(d_rows, 'x', right)  67.6 us
    pallas_call x1, Pallas kernels, attention_backward(): pl.pallas_call(functools.partial(attn_bwd_kernel, seq_len // 2, rows), gr...  58.3 us
    dot_general x8, matrix products, dot(): return jnp.dot(left, right, preferred_element_type=F32)  48.1 us
    ppermute x3, waiting for transfers between devices, device_step(): lax.ppermute(low_sum, 'x', left)  40 us
    pallas_call x1, Pallas kernels, add_rows(): pl.pallas_call(functools.partial(table_kernel, total, counts.shape[0] //...  39.6 us
    ppermute x5, waiting for transfers between devices, ring_blocks(): lax.ppermute(values, axis, left)  38.4 us
    dot_general x4, matrix products, dot_tn(): lax.dot_general(left, right, (((0,), (0,)), ((), ())), preferred_element_...  38.3 us
  transfers between devices with their start and end apart: 60, of which 27 were waited for; matrix products, arithmetic and copies ran while one was open for 28% of the time, Pallas kernels for 17%

commit v1 on v0

--- a/solution.py
+++ b/solution.py
@@ -296,8 +296,8 @@
 
 
 def table_kernel(total, streams, list_ref, count_ref, *refs):
-    blocks, out_ref, rows, bufs, in_sem, out_sem = refs[:-5], refs[-5], refs[-4], refs[-3], refs[-2], refs[-1]
-    span, width = bufs.shape[1:]
+    blocks, outs, (rows, even, odd, in_sem, out_sem) = refs[:-9], refs[-9:-5], refs[-5:]
+    span, width = odd.shape
     loads = []
     first = 0
     for index, block in enumerate(blocks):
@@ -307,15 +307,17 @@
         load.start()
 
     def store(group):
-        return pltpu.make_async_copy(bufs.at[group % 2], out_ref.at[pl.ds(group * span, span), :], out_sem.at[group % 2])
+        return pltpu.make_async_copy(even.at[group % 2], outs[group], out_sem.at[group % 2])
 
     for group in range(4):
-        buf = bufs.at[group % 2]
+        buf = even.at[group % 2]
         if group >= 2:
             store(group - 2).wait()
 
         def clear(step, carry):
-            buf[pl.ds(pl.multiple_of(step * 8, 8), 8), :] = jnp.zeros((8, width), F32)
+            at = pl.ds(pl.multiple_of(step * 8, 8), 8)
+            buf[at, :] = jnp.zeros((8, width), F32)
+            odd[at, :] = jnp.zeros((8, width), F32)
             return carry
 
         lax.fori_loop(0, span // 8, clear, 0, unroll=3 if (span // 8) % 3 == 0 else 1)
@@ -323,28 +325,40 @@
             for load in loads:
                 load.wait()
 
-        for stream in range(streams):
-            slot = stream * 5 + group
-            base = slot * (total // streams)
-
-            def add_row(index):
-                packed = list_ref[base + index]
-                target = packed // total
-                source = packed - target * total
-                buf[pl.ds(target, 1), :] += rows[pl.ds(source, 1), :]
-
-            def add_four(step, carry):
-                for k in range(4):
-                    add_row(step * 4 + k)
+        def add_row(target_buf, stream, index):
+            packed = list_ref[(stream * 5 + group) * (total // streams) + index]
+            target = packed // total
+            source = packed - target * total
+            target_buf[pl.ds(target, 1), :] += rows[pl.ds(source, 1), :]
+
+        for left, right in ((0, 1), (2, 3)):
+            n_left, n_right = count_ref[left * 5 + group], count_ref[right * 5 + group]
+            both = jnp.minimum(n_left, n_right) // 2
+
+            def add_both(step, carry):
+                for k in range(2):
+                    add_row(buf, left, step * 2 + k)
+                    add_row(odd, right, step * 2 + k)
                 return carry
 
-            def add_one(index, carry):
-                add_row(index)
+            def add_left(index, carry):
+                add_row(buf, left, index)
                 return carry
 
-            count = count_ref[slot]
-            lax.fori_loop(0, count // 4, add_four, 0)
-            lax.fori_loop(count // 4 * 4, count, add_one, 0)
+            def add_right(index, carry):
+                add_row(odd, right, index)
+                return carry
+
+            lax.fori_loop(0, both, add_both, 0)
+            lax.fori_loop(both * 2, n_left, add_left, 0)
+            lax.fori_loop(both * 2, n_right, add_right, 0)
+
+        def merge(step, carry):
+            at = pl.ds(pl.multiple_of(step * 8, 8), 8)
+            buf[at, :] += odd[at, :]
+            return carry
+
+        lax.fori_loop(0, span // 8, merge, 0, unroll=3 if (span // 8) % 3 == 0 else 1)
         store(group).start()
     store(2).wait()
     store(3).wait()
@@ -353,16 +367,17 @@
 def add_rows(lists, counts, blocks, vocab):
     width = blocks[0].shape[1]
     total = sum(block.shape[0] for block in blocks)
+    span = vocab // 4
     return pl.pallas_call(
         functools.partial(table_kernel, total, counts.shape[0] // 5),
         grid_spec=pltpu.PrefetchScalarGridSpec(
             num_scalar_prefetch=2,
             grid=(),
             in_specs=[pl.BlockSpec(memory_space=pl.ANY)] * len(blocks),
-            out_specs=pl.BlockSpec(memory_space=pl.ANY),
-            scratch_shapes=[pltpu.VMEM((total, width), F32), pltpu.VMEM((2, vocab // 4, width), F32), pltpu.SemaphoreType.DMA((len(blocks),)), pltpu.SemaphoreType.DMA((2,))],
+            out_specs=[pl.BlockSpec(memory_space=pl.ANY)] * 4,
+            scratch_shapes=[pltpu.VMEM((total, width), F32), pltpu.VMEM((2, span, width), F32), pltpu.VMEM((span, width), F32), pltpu.SemaphoreType.DMA((len(blocks),)), pltpu.SemaphoreType.DMA((2,))],
         ),
-        out_shape=jax.ShapeDtypeStruct((vocab, width), F32),
+        out_shape=[jax.ShapeDtypeStruct((span, width), F32)] * 4,
         compiler_params=pltpu.CompilerParams(vmem_limit_bytes=44 * 1024 * 1024),
         cost_estimate=pl.CostEstimate(flops=30 * vocab * width, bytes_accessed=4 * vocab * width, transcendentals=0),
         name='table_rows',
@@ -633,12 +648,15 @@
         d_b_lin = small[:, at + ffn_cols:at + 2 * ffn_cols].reshape(-1)
         at += 2 * ffn_cols
         d_b_qkv = jnp.concatenate([head_order(small[i, at:at + qkv_cols], pairs_loc) for i in (0, 1)]).reshape(heads_loc, -1)
-        d_table, d_w_qkv, d_w_out, d_w_gate, d_w_lin, d_w_down = lax.optimization_barrier((d_table, d_w_qkv, d_w_out, d_w_gate, d_w_lin, d_w_down))
+        base = jnp.zeros((vocab_loc, width), F32)
+        d_table, base, d_w_qkv, d_w_out, d_w_gate, d_w_lin, d_w_down = lax.optimization_barrier((d_table, base, d_w_qkv, d_w_out, d_w_gate, d_w_lin, d_w_down))
         cols = width // 2
-        base = lax.optimization_barrier(jnp.zeros((vocab_loc, width), F32))
-        other_table = swap(d_table)
-        d_table = lax.dynamic_update_slice_in_dim(base, SHRINK * d_table, ci * cols, 1)
-        d_table = lax.dynamic_update_slice_in_dim(d_table, SHRINK * other_table, (1 - ci) * cols, 1)
+        other_table = [swap(part) for part in d_table]
+        span = vocab_loc // 4
+        for parts, which in ((d_table, ci), (other_table, 1 - ci)):
+            for index, part in enumerate(parts):
+                base = lax.dynamic_update_slice(base, SHRINK * part, (jnp.int32(index * span), which * cols))
+        d_table = base
         return (d_table, d_w_qkv, d_b_qkv, d_w_out, d_b_out, d_ln1_gain, d_ln1_bias, d_w_gate, d_b_gate, d_w_lin, d_b_lin, d_w_down, d_b_down, d_ln2_gain)
 
     return jax.shard_map(device_step, mesh=fine, in_specs=in_specs, out_specs=out_specs, check_vma=False)

time: 1130 us -> 1140 us (level)
  other arithmetic: 118 us -> 133 us
    ppermute x1, waiting for transfers between devices: 0.01 us -> 67.7 us  [device_step(): lax.ppermute(d_rows, 'x', left)]
    ppermute x1, waiting for transfers between devices: 67.6 us -> 0.01 us  [device_step(): lax.ppermute(d_rows, 'x', right)]
    ppermute x3, waiting for transfers between devices: 40 us -> 60 us  [device_step(): lax.ppermute(low_sum, 'x', left)]
    ppermute x3, waiting for transfers between devices: 24.3 us -> 6.2 us  [device_step(): lax.ppermute(top_sum, 'x', right)]
    dynamic_update_slice x2 -> x8, other arithmetic: 27.3 us -> 40.2 us  [device_step(): lax.dynamic_update_slice(base, SHRINK * part, (jnp.int32(index * span), w...]
    reduce_scatter x3, waiting for transfers between devices: 31.6 us -> 19.6 us  [scatter_rows(): return lax.psum_scatter(values, ('z', 'y'), scatter_dimension=1, tiled=True)]
    unnamed x142 -> x130, local copies, waits for them, and re-layouts: 24.8 us -> 24 us
  transfers between devices with their start and end apart: 60 -> 63, of which waited for: 27 -> 31; matrix products, arithmetic and copies ran while one was open for 28% -> 29% of each run, Pallas kernels for 17% -> 17%
where the time goes in v1:
time: 1140 us; the launch traced here: 1130 us
  waiting for transfers between devices  436 us (38%)
  Pallas kernels  216 us (19%)
  local copies, waits for them, and re-layouts  162 us (14%)
  other arithmetic  133 us (12%)
  matrix products  96.6 us (8%)
  starting transfers between devices  69.6 us (6%)
  between operations  16.1 us (1%)
    psum x1, waiting for transfers between devices, device_step(): d_table = lax.psum(d_table, ('z', 'y'))  170 us
    ppermute x1, waiting for transfers between devices, device_step(): lax.ppermute(d_rows, 'x', left)  67.7 us
    ppermute x3, waiting for transfers between devices, device_step(): lax.ppermute(low_sum, 'x', left)  60 us
    pallas_call x1, Pallas kernels, attention_backward(): pl.pallas_call(functools.partial(attn_bwd_kernel, seq_len // 2, rows), gr...  58.4 us
    dot_general x8, matrix products, dot(): return jnp.dot(left, right, preferred_element_type=F32)  48.3 us
    pallas_call x1, Pallas kernels, add_rows(): pl.pallas_call(functools.partial(table_kernel, total, counts.shape[0] //...  47.7 us
    dynamic_update_slice x8, other arithmetic, device_step(): lax.dynamic_update_slice(base, SHRINK * part, (jnp.int32(index * span), w...  40.2 us
    dot_general x4, matrix products, dot_tn(): lax.dot_general(left, right, (((0,), (0,)), ((), ())), preferred_element_...  38.4 us
  transfers between devices with their start and end apart: 63, of which 31 were waited for; matrix products, arithmetic and copies ran while one was open for 29% of the time, Pallas kernels for 17%

profile of v1, /device:TPU:1, one launch (start us, length us, event | category | flops | bytes accessed | tf_op | source)
XLA Modules:
  0.0 1129.4 jit_solution(4929879892855945650)
XLA Ops:
  25.1 15.5 %gather_fusion = bf16[768,1024]{1,0:T(8,128)(2,1)S(1)} fusion(bf16[12576,1024]{1,0:T(8,128)(2,1)} %param.23, s32[1024]{0:T(1024)S(1)} %pad_clamp_fusion.2), kind=kCustom, calls=%fused_computation.4 | custom fusion | bytes 3148800 | tf_op jit(solution)/shard_map/gather | solution.py:484
  52.0 23.3 %gather_fusion.1 = bf16[2304,1024]{1,0:T(8,128)(2,1)} fusion(bf16[12576,1024]{1,0:T(8,128)(2,1)} %param.23, s32[3072]{0:T(1024)S(1)} %pad_clamp_fusion), kind=kCustom, calls=%fused_computation.5 | custom fusion | bytes 9446400 | tf_op jit(solution)/shard_map/gather | solution.py:503
  75.3 10.1 collective-permute-done.7
  88.6 4.1 fusion.15
  98.4 29.1 %collective-permute-done.8 = f32[384,1024]{1,0:T(8,128)S(1)} collective-permute-done((f32[384,1024]{1,0:T(8,128)}, f32[384,1024]{1,0:T(8,128)S(1)}, u32[]{:S(2)}, u32[]{:S(2)}) %collective-permute-start.8) | collective-permute-done | bytes 1572896 | tf_op jit(solution)/shard_map/ppermute | solution.py:516
  128.7 4.1 fusion.14
  139.7 6.1 fusion
  145.8 20.9 %collective-permute-done.9 = f32[384,1024]{1,0:T(8,128)} collective-permute-done((f32[384,1024]{1,0:T(8,128)}, f32[384,1024]{1,0:T(8,128)}, u32[]{:S(2)}, u32[]{:S(2)}) %collective-permute-start.9) | collective-permute-done | bytes 1572896 | tf_op jit(solution)/shard_map/ppermute | solution.py:516
  179.7 4.1 collective-permute-done.10
  186.2 6.9 add_convert_fusion.qkv_ref
  193.1 33.4 %attn_fwd.1 = bf16[1536,512]{1,0:T(8,128)(2,1)S(1)} custom-call(s32[1]{0:T(128)} %bitcast.26.core_ref, bf16[1536,1536]{1,0:T(8,128)(2,1)} %add_convert_fusion.qkv_ref, f32[1536,128]{1,0:T(8,128)S(1)} %get-tuple-element.83.cos_ref, f32[1536,128]{1,0:T(8,128)S(1)} %get-tuple-element.84.sin_ref), custom_call_target="tpu_custom_call" | custom-call | flops 4831838208 | bytes 7077888 | tf_op jit(solution)/shard_map/attn_fwd/pallas_call | solution.py:162
  230.8 4.2 collective-permute-done.13
  257.9 25.7 %geglu_fwd.1 = (bf16[1536,2048]{1,0:T(8,128)(2,1)}, f32[1536,2048]{1,0:T(8,128)}, f32[1536,2048]{1,0:T(8,128)}, bf16[4096,1024]{1,0:T(8,128)(2,1)}) custom-call(bf16[1536,1024]{1,0:T(8,128)(2,1)} %pad_maximum_fusion.3.hidden_ref, f32[16,4,64,1024]{3,2,1,0:T(8,128)} %bitcast.312, f32[1,4096]{1,0:T(1,128)} %bitcast.301), custom_call_target="tpu_custom_call" | custom-call | flops 12884901888 | bytes 31457280 | tf_op jit(solution)/shard_map/geglu_fwd/pallas_call | solution.py:219
  286.4 8.2 fusion.5
  299.1 6.3 fusion.7
  317.6 5.7 collective-permute-done.19
  325.6 19.3 %geglu_bwd.1 = (bf16[1536,4096]{1,0:T(8,128)(2,1)}, f32[1,4096]{1,0:T(1,128)}) custom-call(bf16[1536,1024]{1,0:T(8,128)(2,1)} %pad_maximum_fusion.4.d_ffn_ref, bf16[2048,1024]{1,0:T(8,128)(2,1)} %bitcast.36.weight_ref, f32[1536,2048]{1,0:T(8,128)} %get-tuple-element.95.act_ref, f32[1536,2048]{1,0:T(8,128)} %get-tuple-element.96.slope_ref), custom_call_target="tpu_custom_call" | custom-call | flops 6442450944 | bytes 37748736 | tf_op jit(solution)/shard_map/geglu_bwd/pallas_call | solution.py:250
  344.9 12.0 %fusion.1 = f32[768,1024]{1,0:T(8,128)} fusion(bf16[4096,1024]{1,0:T(8,128)(2,1)} %get-tuple-element.98, bf16[1536,4096]{1,0:T(8,128)(2,1)} %get-tuple-element.97), kind=kOutput, calls=%fused_computation.19 | convolution fusion | flops 6442450944 | bytes 17825792 | tf_op jit(solution)/shard_map/dot_general | solution.py:40
  357.3 10.9 fusion.59
  368.2 11.0 fusion.3
  398.2 58.4 %attn_bwd.1 = (bf16[1536,1536]{1,0:T(8,128)(2,1)}, f32[1,1536]{1,0:T(1,128)}) custom-call(s32[1]{0:T(128)} %bitcast.26.core_ref, bf16[1536,1536]{1,0:T(8,128)(2,1)} %add_convert_fusion.qkv_ref, bf16[1536,512]{1,0:T(8,128)(2,1)} %convolution_convert_fusion.dctx_ref, f32[1536,128]{1,0:T(8,128)} %copy-done.6, f32[1536,128]{1,0:T(8,128)} %copy-done.7), custom_call_target="tpu_custom_call" | custom-call | flops 12079595520 | bytes 11796480 | tf_op jit(solution)/shard_map/attn_bwd/pallas_call | solution.py:182
  457.4 6.2 convolution_add_fusion.1
  475.1 5.2 fusion.11
  480.3 4.9 pad_maximum_fusion
  485.4 20.6 %fusion.60 = f32[4096,1024]{1,0:T(8,128)} fusion(bf16[1536,4096]{1,0:T(8,128)(2,1)} %get-tuple-element.97, bf16[768,1024]{1,0:T(8,128)(2,1)} %copy-done.19, bf16[768,1024]{1,0:T(8,128)(2,1)} %copy-done.14), kind=kOutput, calls=%fused_computation.265 | convolution fusion | flops 12891193344 | bytes 32505856 | tf_op jit(solution)/shard_map/dot_general | solution.py:44
  507.8 67.7 %collective-permute-done.25.refs_2_ = f32[1536,512]{1,0:T(8,128)S(1)} collective-permute-done((f32[1536,512]{1,0:T(8,128)S(1)}, f32[1536,512]{1,0:T(8,128)S(1)}, u32[]{:S(2)}, u32[]{:S(2)}) %collective-permute-start.25) | collective-permute-done | bytes 3145760 | tf_op jit(solution)/shard_map/ppermute | solution.py:593
  584.3 31.5 %bucket_ids.1 = (s32[30720]{0:T(1024)}, s32[20]{0:T(128)}) custom-call(s32[6144]{0:T(1024)} %get-tuple-element.236.group_ref, s32[6144]{0:T(1024)} %get-tuple-element.235.value_ref), custom_call_target="tpu_custom_call" | custom-call | flops 40000000 | bytes 122880 | tf_op jit(solution)/shard_map/bucket_ids/pallas_call | solution.py:288
  622.4 47.7 %table_rows.1 = (f32[3144,512]{1,0:T(8,128)}, f32[3144,512]{1,0:T(8,128)}, f32[3144,512]{1,0:T(8,128)}, f32[3144,512]{1,0:T(8,128)}) custom-call(s32[30720]{0:T(1024)S(1)} %copy-done.8, s32[20]{0:T(128)S(1)} %copy-done.9, f32[1536,512]{1,0:T(8,128)S(1)} %maximum_add_fusion.refs_0_, f32[1536,512]{1,0:T(8,128)S(1)} %copy-done.3, f32[1536,512]{1,0:T(8,128)} %copy-done.18, ...), custom_call_target="tpu_custom_call" | custom-call | flops 193167360 | bytes 25755648 | tf_op jit(solution)/shard_map/table_rows/pallas_call | solution.py:371
  670.1 19.6 %reduce-scatter.6.cloned.1.call-done = f32[4,64,1024]{2,1,0:T(8,128)} async-done(((f32[4,1024,1024]{2,1,0:T(8,128)}), f32[4,64,1024]{2,1,0:T(8,128)}) %reduce-scatter.6.cloned.1.call-update) | async-done | bytes 1048592 | tf_op jit(solution)/shard_map/reduce_scatter | solution.py:565
  721.3 4.5 collective-permute-done.34
  730.4 10.4 collective-permute-done.47
  740.8 5.1 collective-permute-start.49
  754.9 35.7 %collective-permute-done.49 = f32[4,64,1024]{2,1,0:T(8,128)S(1)} collective-permute-done((f32[4,64,1024]{2,1,0:T(8,128)S(1)}, f32[4,64,1024]{2,1,0:T(8,128)S(1)}, u32[]{:S(2)}, u32[]{:S(2)}) %collective-permute-start.49) | collective-permute-done | bytes 1048608 | tf_op jit(solution)/shard_map/ppermute | solution.py:394
  801.1 15.1 %collective-permute-done.51 = f32[2,64,1024]{2,1,0:T(8,128)S(1)} collective-permute-done((f32[2,64,1024]{2,1,0:T(8,128)S(1)}, f32[2,64,1024]{2,1,0:T(8,128)S(1)}, u32[]{:S(2)}, u32[]{:S(2)}) %collective-permute-start.51) | collective-permute-done | bytes 524320 | tf_op jit(solution)/shard_map/ppermute | solution.py:397
  830.2 4.7 collective-permute-start.41
  838.6 4.9 broadcast_in_dim.296
  843.6 5.4 bitcast_dynamic-update-slice_fusion.1
  851.7 4.2 fusion.71
  855.8 5.4 copy.73
  861.2 5.3 copy.72
  866.6 6.4 bitcast_dynamic-update-slice_fusion
  873.0 4.9 slice.331
  883.6 170.4 %all-reduce.7.cloned.1.call-done = (f32[3144,512]{1,0:T(8,128)}, f32[3144,512]{1,0:T(8,128)}, f32[3144,512]{1,0:T(8,128)}, f32[3144,512]{1,0:T(8,128)}) async-done(((f32[3144,512]{1,0:T(8,128)}, f32[3144,512]{1,0:T(8,128)}, f32[3144,512]{1,0:T(8,128)}, f32[3144,512]{1,0:T(8,128)}), (f32[3144,512]{1,0:T(8,128)}, f32[3144,512]{1,0:T(8,128)}, f32[3144,512]{1,0:T(8,128)}, ...) | async-done | bytes 25755664 | tf_op jit(solution)/shard_map/psum | solution.py:621
  1065.2 16.9 %broadcast_in_dim.295 = f32[12576,1024]{1,0:T(8,128)} broadcast(f32[]{:T(128)} %constant.456.clone.1), dimensions={} | broadcast | bytes 51511300 | tf_op jit(solution)/shard_map/broadcast_in_dim | solution.py:651
  1082.1 6.6 multiply_dynamic-update-slice_fusion.7
  1088.7 6.6 multiply_dynamic-update-slice_fusion.6
  1102.4 6.4 multiply_dynamic-update-slice_fusion.3
  1108.8 6.4 multiply_dynamic-update-slice_fusion.2
  (430 shorter events, 265.7 us)
Async XLA Ops:
  7.2 128.7 %all-gather.3.cloned.1.call-start = ((), (), s32[]{:S(2)}) async-start(), calls=%async_computation.3 | async-start | bytes 11141120 | tf_op jit(solution)/shard_map/all_gather | solution.py:490
  15.6 25.0 %collective-permute-start.3 = (f32[104,1024]{1,0:T(8,128)S(1)}, f32[104,1024]{1,0:T(8,128)S(1)}, u32[]{:S(2)}, u32[]{:S(2)}) collective-permute-start(f32[104,1024]{1,0:T(8,128)S(1)} %pad_maximum_fusion.10), channel_id=1, source_target_pairs={{0,64},{32,96},{64,0},{96,32},{1,65},{33,97},{65,1},{97,33},{2,66}... | collective-permute-start | bytes 1277960 | tf_op jit(solution)/shard_map/ppermute | solution.py:399
  19.2 21.4 %collective-permute-start.2 = (f32[104,1024]{1,0:T(8,128)S(1)}, f32[104,1024]{1,0:T(8,128)S(1)}, u32[]{:S(2)}, u32[]{:S(2)}) collective-permute-start(f32[104,1024]{1,0:T(8,128)S(1)} %pad_maximum_fusion.10), channel_id=1, source_target_pairs={{0,96},{32,0},{64,32},{96,64},{1,97},{33,1},{65,33},{97,65},{2,98}... | collective-permute-start | bytes 1277960 | tf_op jit(solution)/shard_map/ppermute | solution.py:394
  20.1 22.0 %collective-permute-start.1 = (f32[104,1024]{1,0:T(8,128)S(1)}, f32[104,1024]{1,0:T(8,128)}, u32[]{:S(2)}, u32[]{:S(2)}) collective-permute-start(f32[104,1024]{1,0:T(8,128)S(1)} %pad_maximum_fusion.10), channel_id=1, source_target_pairs={{0,32},{32,64},{64,96},{96,0},{1,33},{33,65},{65,97},{97,1},{2,34}... | collective-permute-start | bytes 1277960 | tf_op jit(solution)/shard_map/ppermute | solution.py:394
  45.5 212.4 %all-gather.5.cloned.1.call-start = ((), (), s32[]{:S(2)}) async-start(), calls=%async_computation.4 | async-start | bytes 17825792 | tf_op jit(solution)/shard_map/all_gather | solution.py:490
  46.6 623.4 %reduce-scatter.4.cloned.1.call-start = ((), (), s32[]{:S(2)}) async-start(), calls=%async_computation.5 | async-start | bytes 8912896 | tf_op jit(solution)/shard_map/reduce_scatter | solution.py:565
  49.4 35.9 %collective-permute-start.7 = (f32[384,1024]{1,0:T(8,128)}, f32[384,1024]{1,0:T(8,128)S(1)}, u32[]{:S(2)}, u32[]{:S(2)}) collective-permute-start(f32[384,1024]{1,0:T(8,128)} %get-tuple-element.217), channel_id=1, source_target_pairs={{0,96},{32,0},{64,32},{96,64},{1,97},{33,1},{65,33},{97,65},{2,98}... | collective-permute-start | bytes 4718600 | tf_op jit(solution)/shard_map/ppermute | solution.py:516
  51.5 37.1 %collective-permute-start.4 = (f32[384,1024]{1,0:T(8,128)S(1)}, f32[384,1024]{1,0:T(8,128)}, u32[]{:S(2)}, u32[]{:S(2)}) collective-permute-start(f32[384,1024]{1,0:T(8,128)S(1)} %get-tuple-element.218), channel_id=1, source_target_pairs={{0,32},{32,64},{64,96},{96,0},{1,33},{33,65},{65,97},{97,1},{2,34}... | collective-permute-start | bytes 4718600 | tf_op jit(solution)/shard_map/ppermute | solution.py:516
  92.7 34.8 %collective-permute-start.8 = (f32[384,1024]{1,0:T(8,128)}, f32[384,1024]{1,0:T(8,128)S(1)}, u32[]{:S(2)}, u32[]{:S(2)}) collective-permute-start(f32[384,1024]{1,0:T(8,128)} %get-tuple-element.210), channel_id=1, source_target_pairs={{0,96},{32,0},{64,32},{96,64},{1,97},{33,1},{65,33},{97,65},{2,98}... | collective-permute-start | bytes 4718600 | tf_op jit(solution)/shard_map/ppermute | solution.py:516
  92.7 36.0 %collective-permute-start.5 = (f32[384,1024]{1,0:T(8,128)}, f32[384,1024]{1,0:T(8,128)}, u32[]{:S(2)}, u32[]{:S(2)}) collective-permute-start(f32[384,1024]{1,0:T(8,128)} %get-tuple-element.211), channel_id=1, source_target_pairs={{0,32},{32,64},{64,96},{96,0},{1,33},{33,65},{65,97},{97,1},{2,34}... | collective-permute-start | bytes 4718600 | tf_op jit(solution)/shard_map/ppermute | solution.py:516
  132.8 33.9 %collective-permute-start.9 = (f32[384,1024]{1,0:T(8,128)}, f32[384,1024]{1,0:T(8,128)}, u32[]{:S(2)}, u32[]{:S(2)}) collective-permute-start(f32[384,1024]{1,0:T(8,128)} %get-tuple-element.208), channel_id=1, source_target_pairs={{0,96},{32,0},{64,32},{96,64},{1,97},{33,1},{65,33},{97,65},{2,98}... | collective-permute-start | bytes 4718600 | tf_op jit(solution)/shard_map/ppermute | solution.py:516
  133.0 35.4 %collective-permute-start.6 = (f32[384,1024]{1,0:T(8,128)}, f32[384,1024]{1,0:T(8,128)}, u32[]{:S(2)}, u32[]{:S(2)}) collective-permute-start(f32[384,1024]{1,0:T(8,128)} %get-tuple-element.209), channel_id=1, source_target_pairs={{0,32},{32,64},{64,96},{96,0},{1,33},{33,65},{65,97},{97,1},{2,34}... | collective-permute-start | bytes 4718600 | tf_op jit(solution)/shard_map/ppermute | solution.py:516
  178.2 48.4 %collective-permute-start.12 = (f32[512,1024]{1,0:T(8,128)}, f32[512,1024]{1,0:T(8,128)}, u32[]{:S(2)}, u32[]{:S(2)}) collective-permute-start(f32[512,1024]{1,0:T(8,128)} %dynamic-slice_convert_fusion), channel_id=1, source_target_pairs={{0,96},{32,0},{64,32},{96,64},{1,97},{33,1},{65,33},{97,65},{2,98}... | collective-permute-start | bytes 6291464 | tf_op jit(solution)/shard_map/ppermute | solution.py:526
  178.7 48.4 %collective-permute-start.11 = (f32[512,1024]{1,0:T(8,128)}, f32[512,1024]{1,0:T(8,128)}, u32[]{:S(2)}, u32[]{:S(2)}) collective-permute-start(f32[512,1024]{1,0:T(8,128)} %dynamic-slice_convert_fusion), channel_id=1, source_target_pairs={{0,32},{32,64},{64,96},{96,0},{1,33},{33,65},{65,97},{97,1},{2,34}... | collective-permute-start | bytes 6291464 | tf_op jit(solution)/shard_map/ppermute | solution.py:526
  236.7 17.5 %collective-permute-start.14 = (f32[768,1024]{1,0:T(8,128)S(1)}, f32[768,1024]{1,0:T(8,128)S(1)}, u32[]{:S(2)}, u32[]{:S(2)}) collective-permute-start(f32[768,1024]{1,0:T(8,128)S(1)} %get-tuple-element.192), channel_id=1, source_target_pairs={{0,1},{1,0},{2,3},{3,2},{4,5},{5,4},{6,7},{7,6},{8,9},{9,8},{10,11... | collective-permute-start | bytes 9437192 | tf_op jit(solution)/shard_map/ppermute | solution.py:21
  247.2 36.4 %collective-permute-start.16 = (f32[256,1024]{1,0:T(8,128)}, f32[256,1024]{1,0:T(8,128)}, u32[]{:S(2)}, u32[]{:S(2)}) collective-permute-start(f32[256,1024]{1,0:T(8,128)} %slice.243), channel_id=1, source_target_pairs={{0,96},{32,0},{64,32},{96,64},{1,97},{33,1},{65,33},{97,65},{2,98}... | collective-permute-start | bytes 3145736 | tf_op jit(solution)/shard_map/ppermute | solution.py:548
  247.2 36.4 %collective-permute-start.15 = (f32[256,1024]{1,0:T(8,128)}, f32[256,1024]{1,0:T(8,128)}, u32[]{:S(2)}, u32[]{:S(2)}) collective-permute-start(f32[256,1024]{1,0:T(8,128)} %slice.242), channel_id=1, source_target_pairs={{0,32},{32,64},{64,96},{96,0},{1,33},{33,65},{65,97},{97,1},{2,34}... | collective-permute-start | bytes 3145736 | tf_op jit(solution)/shard_map/ppermute | solution.py:548
  294.6 10.8 collective-permute-start.18
  357.0 22.3 %collective-permute-start.20 = (f32[768,1024]{1,0:T(8,128)}, f32[768,1024]{1,0:T(8,128)}, u32[]{:S(2)}, u32[]{:S(2)}) collective-permute-start(f32[768,1024]{1,0:T(8,128)} %fusion.1), channel_id=1, source_target_pairs={{0,1},{1,0},{2,3},{3,2},{4,5},{5,4},{6,7},{7,6},{8,9},{9,8},{10,11... | collective-permute-start | bytes 9437192 | tf_op jit(solution)/shard_map/ppermute | solution.py:21
  368.2 301.9 %reduce-scatter.8.cloned.1.call-start = ((), (), s32[]{:S(2)}) async-start(), calls=%async_computation.7 | async-start | bytes 11141120 | tf_op jit(solution)/shard_map/reduce_scatter | solution.py:565
  485.2 204.5 %reduce-scatter.6.cloned.1.call-start = ((), (), s32[]{:S(2)}) async-start(), calls=%async_computation.6 | async-start | bytes 17825792 | tf_op jit(solution)/shard_map/reduce_scatter | solution.py:565
  506.1 547.9 %all-reduce.7.cloned.1.call-start = ((), (), s32[]{:S(2)}) async-start(), calls=%async_computation.8 | async-start | bytes 51511296 | tf_op jit(solution)/shard_map/psum | solution.py:621
  506.1 69.4 %collective-permute-start.25 = (f32[1536,512]{1,0:T(8,128)S(1)}, f32[1536,512]{1,0:T(8,128)S(1)}, u32[]{:S(2)}, u32[]{:S(2)}) collective-permute-start(f32[1536,512]{1,0:T(8,128)S(1)} %maximum_add_fusion.refs_0_), channel_id=1, source_target_pairs={{0,96},{32,0},{64,32},{96,64},{1,97},{33,1},{65,33},{97,65},{2,98}... | collective-permute-start | bytes 9437192 | tf_op jit(solution)/shard_map/ppermute | solution.py:593
  507.8 72.0 %collective-permute-start.24 = (f32[1536,512]{1,0:T(8,128)S(1)}, f32[1536,512]{1,0:T(8,128)S(1)}, u32[]{:S(2)}, u32[]{:S(2)}) collective-permute-start(f32[1536,512]{1,0:T(8,128)S(1)} %maximum_add_fusion.refs_0_), channel_id=1, source_target_pairs={{0,32},{32,64},{64,96},{96,0},{1,33},{33,65},{65,97},{97,1},{2,34}... | collective-permute-start | bytes 9437192 | tf_op jit(solution)/shard_map/ppermute | solution.py:593
  576.9 38.9 %collective-permute-start.27 = (f32[768,512]{1,0:T(8,128)}, f32[768,512]{1,0:T(8,128)}, u32[]{:S(2)}, u32[]{:S(2)}) collective-permute-start(f32[768,512]{1,0:T(8,128)} %slice.320), channel_id=1, source_target_pairs={{0,96},{32,0},{64,32},{96,64},{1,97},{33,1},{65,33},{97,65},{2,98}... | collective-permute-start | bytes 4718600 | tf_op jit(solution)/shard_map/ppermute | solution.py:617
  582.7 36.1 %collective-permute-start.26 = (f32[768,512]{1,0:T(8,128)}, f32[768,512]{1,0:T(8,128)}, u32[]{:S(2)}, u32[]{:S(2)}) collective-permute-start(f32[768,512]{1,0:T(8,128)} %slice.319), channel_id=1, source_target_pairs={{0,32},{32,64},{64,96},{96,0},{1,33},{33,65},{65,97},{97,1},{2,34}... | collective-permute-start | bytes 4718600 | tf_op jit(solution)/shard_map/ppermute | solution.py:616
  698.2 15.3 %collective-permute-start.42 = (f32[64,1024]{1,0:T(8,128)S(1)}, f32[64,1024]{1,0:T(8,128)S(1)}, u32[]{:S(2)}, u32[]{:S(2)}) collective-permute-start(f32[64,1024]{1,0:T(8,128)S(1)} %get-tuple-element.226), channel_id=1, source_target_pairs={{0,32},{32,64},{64,96},{96,0},{1,33},{33,65},{65,97},{97,1},{2,34}... | collective-permute-start | bytes 786440 | tf_op jit(solution)/shard_map/ppermute | solution.py:610
  699.9 16.3 %collective-permute-start.44 = (f32[64,1024]{1,0:T(8,128)S(1)}, f32[64,1024]{1,0:T(8,128)S(1)}, u32[]{:S(2)}, u32[]{:S(2)}) collective-permute-start(f32[64,1024]{1,0:T(8,128)S(1)} %get-tuple-element.227), channel_id=1, source_target_pairs={{0,96},{32,0},{64,32},{96,64},{1,97},{33,1},{65,33},{97,65},{2,98}... | collective-permute-start | bytes 786440 | tf_op jit(solution)/shard_map/ppermute | solution.py:610
  704.3 13.8 %collective-permute-start.43 = (f32[64,1024]{1,0:T(8,128)S(1)}, f32[64,1024]{1,0:T(8,128)S(1)}, u32[]{:S(2)}, u32[]{:S(2)}) collective-permute-start(f32[64,1024]{1,0:T(8,128)S(1)} %get-tuple-element.228), channel_id=1, source_target_pairs={{0,64},{32,96},{64,0},{96,32},{1,65},{33,97},{65,1},{97,33},{2,66}... | collective-permute-start | bytes 786440 | tf_op jit(solution)/shard_map/ppermute | solution.py:610
  707.0 38.9 %collective-permute-start.35 = (f32[72,1024]{1,0:T(8,128)S(1)}, f32[72,1024]{1,0:T(8,128)S(1)}, u32[]{:S(2)}, u32[]{:S(2)}) collective-permute-start(f32[72,1024]{1,0:T(8,128)S(1)} %pad_maximum_fusion.11), channel_id=1, source_target_pairs={{0,6},{2,0},{4,2},{6,4},{1,7},{3,1},{5,3},{7,5},{8,14},{10,8},{12,... | collective-permute-start | bytes 884744 | tf_op jit(solution)/shard_map/ppermute | solution.py:394
  709.7 16.1 %collective-permute-start.34 = (f32[72,1024]{1,0:T(8,128)S(1)}, f32[72,1024]{1,0:T(8,128)S(1)}, u32[]{:S(2)}, u32[]{:S(2)}) collective-permute-start(f32[72,1024]{1,0:T(8,128)S(1)} %pad_maximum_fusion.11), channel_id=1, source_target_pairs={{0,2},{2,4},{4,6},{6,0},{1,3},{3,5},{5,7},{7,1},{8,10},{10,12},{12... | collective-permute-start | bytes 884744 | tf_op jit(solution)/shard_map/ppermute | solution.py:394
  713.5 32.4 %collective-permute-start.36 = (f32[72,1024]{1,0:T(8,128)S(1)}, f32[72,1024]{1,0:T(8,128)S(1)}, u32[]{:S(2)}, u32[]{:S(2)}) collective-permute-start(f32[72,1024]{1,0:T(8,128)S(1)} %pad_maximum_fusion.11), channel_id=1, source_target_pairs={{0,4},{2,6},{4,0},{6,2},{1,5},{3,7},{5,1},{7,3},{8,12},{10,14},{12... | collective-permute-start | bytes 884744 | tf_op jit(solution)/shard_map/ppermute | solution.py:399
  718.3 12.0 %collective-permute-start.45 = (f32[64,1024]{1,0:T(8,128)S(1)}, f32[64,1024]{1,0:T(8,128)S(1)}, u32[]{:S(2)}, u32[]{:S(2)}) collective-permute-start(f32[64,1024]{1,0:T(8,128)S(1)} %get-tuple-element.176), channel_id=1, source_target_pairs={{0,8},{8,16},{16,24},{24,0},{1,9},{9,17},{17,25},{25,1},{2,10},{10... | collective-permute-start | bytes 786440 | tf_op jit(solution)/shard_map/ppermute | solution.py:394
  725.8 15.0 %collective-permute-start.47 = (f32[64,1024]{1,0:T(8,128)S(1)}, f32[64,1024]{1,0:T(8,128)S(1)}, u32[]{:S(2)}, u32[]{:S(2)}) collective-permute-start(f32[64,1024]{1,0:T(8,128)S(1)} %get-tuple-element.176), channel_id=1, source_target_pairs={{0,16},{8,24},{16,0},{24,8},{1,17},{9,25},{17,1},{25,9},{2,18},{10... | collective-permute-start | bytes 786440 | tf_op jit(solution)/shard_map/ppermute | solution.py:399
  740.8 49.8 %collective-permute-start.49 = (f32[4,64,1024]{2,1,0:T(8,128)S(1)}, f32[4,64,1024]{2,1,0:T(8,128)S(1)}, u32[]{:S(2)}, u32[]{:S(2)}) collective-permute-start(f32[4,64,1024]{2,1,0:T(8,128)S(1)} %bitcast_dynamic-update-slice_fusion.17), channel_id=1, source_target_pairs={{0,6},{2,0},{4,2},{6,4},{1,7},{3,1},{5,3},{7,5},{8,14},{10,8},{12,... | collective-permute-start | bytes 3145736 | tf_op jit(solution)/shard_map/ppermute | solution.py:394
  745.9 48.3 %collective-permute-start.48 = (f32[4,64,1024]{2,1,0:T(8,128)S(1)}, f32[4,64,1024]{2,1,0:T(8,128)S(1)}, u32[]{:S(2)}, u32[]{:S(2)}) collective-permute-start(f32[4,64,1024]{2,1,0:T(8,128)S(1)} %bitcast_dynamic-update-slice_fusion.17), channel_id=1, source_target_pairs={{0,2},{2,4},{4,6},{6,0},{1,3},{3,5},{5,7},{7,1},{8,10},{10,12},{12... | collective-permute-start | bytes 3145736 | tf_op jit(solution)/shard_map/ppermute | solution.py:394
  746.0 52.6 %collective-permute-start.38 = (f32[4,72,1024]{2,1,0:T(8,128)S(1)}, f32[4,72,1024]{2,1,0:T(8,128)S(1)}, u32[]{:S(2)}, u32[]{:S(2)}) collective-permute-start(f32[4,72,1024]{2,1,0:T(8,128)S(1)} %bitcast_dynamic-update-slice_fusion.13), channel_id=1, source_target_pairs={{0,24},{8,0},{16,8},{24,16},{1,25},{9,1},{17,9},{25,17},{2,26},{10... | collective-permute-start | bytes 3538952 | tf_op jit(solution)/shard_map/ppermute | solution.py:394
  747.2 53.7 %collective-permute-start.37 = (f32[4,72,1024]{2,1,0:T(8,128)S(1)}, f32[4,72,1024]{2,1,0:T(8,128)S(1)}, u32[]{:S(2)}, u32[]{:S(2)}) collective-permute-start(f32[4,72,1024]{2,1,0:T(8,128)S(1)} %bitcast_dynamic-update-slice_fusion.13), channel_id=1, source_target_pairs={{0,8},{8,16},{16,24},{24,0},{1,9},{9,17},{17,25},{25,1},{2,10},{10... | collective-permute-start | bytes 3538952 | tf_op jit(solution)/shard_map/ppermute | solution.py:394
  790.6 25.6 %collective-permute-start.51 = (f32[2,64,1024]{2,1,0:T(8,128)S(1)}, f32[2,64,1024]{2,1,0:T(8,128)S(1)}, u32[]{:S(2)}, u32[]{:S(2)}) collective-permute-start(f32[2,64,1024]{2,1,0:T(8,128)S(1)} %slice.328), channel_id=1, source_target_pairs={{0,6},{2,0},{4,2},{6,4},{1,7},{3,1},{5,3},{7,5},{8,14},{10,8},{12,... | collective-permute-start | bytes 1572872 | tf_op jit(solution)/shard_map/ppermute | solution.py:397
  794.2 25.5 %collective-permute-start.50 = (f32[2,64,1024]{2,1,0:T(8,128)S(1)}, f32[2,64,1024]{2,1,0:T(8,128)S(1)}, u32[]{:S(2)}, u32[]{:S(2)}) collective-permute-start(f32[2,64,1024]{2,1,0:T(8,128)S(1)} %slice.327), channel_id=1, source_target_pairs={{0,2},{2,4},{4,6},{6,0},{1,3},{3,5},{5,7},{7,1},{8,10},{10,12},{12... | collective-permute-start | bytes 1572872 | tf_op jit(solution)/shard_map/ppermute | solution.py:397
  798.6 28.2 %collective-permute-start.40 = (f32[2,72,1024]{2,1,0:T(8,128)S(1)}, f32[2,72,1024]{2,1,0:T(8,128)S(1)}, u32[]{:S(2)}, u32[]{:S(2)}) collective-permute-start(f32[2,72,1024]{2,1,0:T(8,128)S(1)} %slice.322), channel_id=1, source_target_pairs={{0,24},{8,0},{16,8},{24,16},{1,25},{9,1},{17,9},{25,17},{2,26},{10... | collective-permute-start | bytes 1769480 | tf_op jit(solution)/shard_map/ppermute | solution.py:397
  801.0 28.1 %collective-permute-start.39 = (f32[2,72,1024]{2,1,0:T(8,128)S(1)}, f32[2,72,1024]{2,1,0:T(8,128)S(1)}, u32[]{:S(2)}, u32[]{:S(2)}) collective-permute-start(f32[2,72,1024]{2,1,0:T(8,128)S(1)} %slice.321), channel_id=1, source_target_pairs={{0,8},{8,16},{16,24},{24,0},{1,9},{9,17},{17,25},{25,1},{2,10},{10... | collective-permute-start | bytes 1769480 | tf_op jit(solution)/shard_map/ppermute | solution.py:397
  820.8 28.1 %collective-permute-start.52 = (f32[16,64,1024]{2,1,0:T(8,128)}, f32[16,64,1024]{2,1,0:T(8,128)}, u32[]{:S(2)}, u32[]{:S(2)}) collective-permute-start(f32[16,64,1024]{2,1,0:T(8,128)} %bitcast.87), channel_id=1, source_target_pairs={{0,1},{1,0},{2,3},{3,2},{4,5},{5,4},{6,7},{7,6},{8,9},{9,8},{10,11... | collective-permute-start | bytes 12582920 | tf_op jit(solution)/shard_map/ppermute | solution.py:21
  830.2 36.4 %collective-permute-start.41 = (f32[16,72,1024]{2,1,0:T(8,128)}, f32[16,72,1024]{2,1,0:T(8,128)}, u32[]{:S(2)}, u32[]{:S(2)}) collective-permute-start(f32[16,72,1024]{2,1,0:T(8,128)} %bitcast.58), channel_id=1, source_target_pairs={{0,1},{1,0},{2,3},{3,2},{4,5},{5,4},{6,7},{7,6},{8,9},{9,8},{10,11... | collective-permute-start | bytes 14155784 | tf_op jit(solution)/shard_map/ppermute | solution.py:21
  1054.0 48.5 %collective-permute-start.53 = (f32[3144,512]{1,0:T(8,128)}, f32[3144,512]{1,0:T(8,128)}, u32[]{:S(2)}, u32[]{:S(2)}) collective-permute-start(f32[3144,512]{1,0:T(8,128)} %get-tuple-element.119), channel_id=1, source_target_pairs={{0,1},{1,0},{2,3},{3,2},{4,5},{5,4},{6,7},{7,6},{8,9},{9,8},{10,11... | collective-permute-start | bytes 19316744 | tf_op jit(solution)/shard_map/ppermute | solution.py:21
  1064.5 44.3 %collective-permute-start.54 = (f32[3144,512]{1,0:T(8,128)}, f32[3144,512]{1,0:T(8,128)}, u32[]{:S(2)}, u32[]{:S(2)}) collective-permute-start(f32[3144,512]{1,0:T(8,128)} %get-tuple-element.120), channel_id=1, source_target_pairs={{0,1},{1,0},{2,3},{3,2},{4,5},{5,4},{6,7},{7,6},{8,9},{9,8},{10,11... | collective-permute-start | bytes 19316744 | tf_op jit(solution)/shard_map/ppermute | solution.py:21
  1064.5 50.7 %collective-permute-start.55 = (f32[3144,512]{1,0:T(8,128)}, f32[3144,512]{1,0:T(8,128)S(1)}, u32[]{:S(2)}, u32[]{:S(2)}) collective-permute-start(f32[3144,512]{1,0:T(8,128)} %get-tuple-element.121), channel_id=1, source_target_pairs={{0,1},{1,0},{2,3},{3,2},{4,5},{5,4},{6,7},{7,6},{8,9},{9,8},{10,11... | collective-permute-start | bytes 19316744 | tf_op jit(solution)/shard_map/ppermute | solution.py:21
  1065.0 53.8 %collective-permute-start.56 = (f32[3144,512]{1,0:T(8,128)}, f32[3144,512]{1,0:T(8,128)S(1)}, u32[]{:S(2)}, u32[]{:S(2)}) collective-permute-start(f32[3144,512]{1,0:T(8,128)} %get-tuple-element.122), channel_id=1, source_target_pairs={{0,1},{1,0},{2,3},{3,2},{4,5},{5,4},{6,7},{7,6},{8,9},{9,8},{10,11... | collective-permute-start | bytes 19316744 | tf_op jit(solution)/shard_map/ppermute | solution.py:21
  (70 other events, 778.2 us)
Sparse Core Ops, SparseCore 0:
  45.6 81.6 all-gather.2
  129.4 110.9 all-gather.4
  368.3 85.2 reduce-scatter.3
  485.3 89.5 reduce-scatter.7
  578.7 110.9 reduce-scatter.5
  693.9 360.0 all-reduce.6

commit v2 on v0

--- a/solution.py
+++ b/solution.py
@@ -278,12 +278,16 @@
     lax.fori_loop(0, size, place, 0)
 
 
+def index_bits(total):
+    return (total - 1).bit_length()
+
+
 def bucket_ids(ids, streams, vocab):
     total = ids.shape[0]
     size = total // streams
     span = vocab // 4
     group = jnp.where(ids < 0, 4, ids // span)
-    value = jnp.where(ids < 0, 0, (ids % span) * total + jnp.arange(total, dtype=jnp.int32))
+    value = jnp.where(ids < 0, 0, (ids % span) * (1 << index_bits(total)) + jnp.arange(total, dtype=jnp.int32))
     smem = pl.BlockSpec(memory_space=pltpu.SMEM)
     return pl.pallas_call(
         functools.partial(bucket_kernel, streams),
@@ -296,8 +300,9 @@
 
 
 def table_kernel(total, streams, list_ref, count_ref, *refs):
-    blocks, out_ref, rows, bufs, in_sem, out_sem = refs[:-5], refs[-5], refs[-4], refs[-3], refs[-2], refs[-1]
+    blocks, outs, (rows, bufs, in_sem, out_sem) = refs[:-8], refs[-8:-4], refs[-4:]
     span, width = bufs.shape[1:]
+    bits = index_bits(total)
     loads = []
     first = 0
     for index, block in enumerate(blocks):
@@ -307,7 +312,7 @@
         load.start()
 
     def store(group):
-        return pltpu.make_async_copy(bufs.at[group % 2], out_ref.at[pl.ds(group * span, span), :], out_sem.at[group % 2])
+        return pltpu.make_async_copy(bufs.at[group % 2], outs[group], out_sem.at[group % 2])
 
     for group in range(4):
         buf = bufs.at[group % 2]
@@ -325,12 +330,12 @@
 
         for stream in range(streams):
             slot = stream * 5 + group
-            base = slot * (total // streams)
+            first_entry = slot * (total // streams)
 
             def add_row(index):
-                packed = list_ref[base + index]
-                target = packed // total
-                source = packed - target * total
+                packed = list_ref[first_entry + index]
+                target = lax.shift_right_logical(packed, bits)
+                source = packed & ((1 << bits) - 1)
                 buf[pl.ds(target, 1), :] += rows[pl.ds(source, 1), :]
 
             def add_four(step, carry):
@@ -343,8 +348,9 @@
                 return carry
 
             count = count_ref[slot]
-            lax.fori_loop(0, count // 4, add_four, 0)
-            lax.fori_loop(count // 4 * 4, count, add_one, 0)
+            quads = lax.shift_right_logical(count, 2)
+            lax.fori_loop(0, quads, add_four, 0)
+            lax.fori_loop(quads * 4, count, add_one, 0)
         store(group).start()
     store(2).wait()
     store(3).wait()
@@ -353,16 +359,17 @@
 def add_rows(lists, counts, blocks, vocab):
     width = blocks[0].shape[1]
     total = sum(block.shape[0] for block in blocks)
+    span = vocab // 4
     return pl.pallas_call(
         functools.partial(table_kernel, total, counts.shape[0] // 5),
         grid_spec=pltpu.PrefetchScalarGridSpec(
             num_scalar_prefetch=2,
             grid=(),
             in_specs=[pl.BlockSpec(memory_space=pl.ANY)] * len(blocks),
-            out_specs=pl.BlockSpec(memory_space=pl.ANY),
-            scratch_shapes=[pltpu.VMEM((total, width), F32), pltpu.VMEM((2, vocab // 4, width), F32), pltpu.SemaphoreType.DMA((len(blocks),)), pltpu.SemaphoreType.DMA((2,))],
+            out_specs=[pl.BlockSpec(memory_space=pl.ANY)] * 4,
+            scratch_shapes=[pltpu.VMEM((total, width), F32), pltpu.VMEM((2, span, width), F32), pltpu.SemaphoreType.DMA((len(blocks),)), pltpu.SemaphoreType.DMA((2,))],
         ),
-        out_shape=jax.ShapeDtypeStruct((vocab, width), F32),
+        out_shape=[jax.ShapeDtypeStruct((span, width), F32)] * 4,
         compiler_params=pltpu.CompilerParams(vmem_limit_bytes=44 * 1024 * 1024),
         cost_estimate=pl.CostEstimate(flops=30 * vocab * width, bytes_accessed=4 * vocab * width, transcendentals=0),
         name='table_rows',
@@ -633,12 +640,15 @@
         d_b_lin = small[:, at + ffn_cols:at + 2 * ffn_cols].reshape(-1)
         at += 2 * ffn_cols
         d_b_qkv = jnp.concatenate([head_order(small[i, at:at + qkv_cols], pairs_loc) for i in (0, 1)]).reshape(heads_loc, -1)
-        d_table, d_w_qkv, d_w_out, d_w_gate, d_w_lin, d_w_down = lax.optimization_barrier((d_table, d_w_qkv, d_w_out, d_w_gate, d_w_lin, d_w_down))
+        base = jnp.zeros((vocab_loc, width), F32)
+        d_table, d_w_gate, d_w_lin, d_w_down = lax.optimization_barrier((d_table, d_w_gate, d_w_lin, d_w_down))
         cols = width // 2
-        base = lax.optimization_barrier(jnp.zeros((vocab_loc, width), F32))
-        other_table = swap(d_table)
-        d_table = lax.dynamic_update_slice_in_dim(base, SHRINK * d_table, ci * cols, 1)
-        d_table = lax.dynamic_update_slice_in_dim(d_table, SHRINK * other_table, (1 - ci) * cols, 1)
+        other_table = [swap(part) for part in d_table]
+        span = vocab_loc // 4
+        for parts, which in ((d_table, ci), (other_table, 1 - ci)):
+            for index, part in enumerate(parts):
+                base = lax.dynamic_update_slice(base, SHRINK * part, (jnp.int32(index * span), which * cols))
+        d_table = base
         return (d_table, d_w_qkv, d_b_qkv, d_w_out, d_b_out, d_ln1_gain, d_ln1_bias, d_w_gate, d_b_gate, d_w_lin, d_b_lin, d_w_down, d_b_down, d_ln2_gain)
 
     return jax.shard_map(device_step, mesh=fine, in_specs=in_specs, out_specs=out_specs, check_vma=False)

time: 1130 us -> 1140 us (level)
  other arithmetic: 118 us -> 131 us
  Pallas kernels: 208 us -> 196 us
    ppermute x3, waiting for transfers between devices: 40 us -> 0.01 us  [device_step(): lax.ppermute(low_sum, 'x', left)]
    ppermute x5, waiting for transfers between devices: 5.47 us -> 44.8 us  [ring_blocks(): lax.ppermute(values, axis, right)]
    ppermute x5, waiting for transfers between devices: 38.4 us -> 0.01 us  [ring_blocks(): lax.ppermute(values, axis, left)]
    ppermute x3, waiting for transfers between devices: 24.3 us -> 61.4 us  [device_step(): lax.ppermute(top_sum, 'x', right)]
    ppermute x2, waiting for transfers between devices: 15.5 us -> 0.3 us  [ring_blocks(): lax.ppermute(from_right[mid:], axis, left)]
    ppermute x2, waiting for transfers between devices: 3.72 us -> 18 us  [ring_blocks(): lax.ppermute(from_left[:mid], axis, right)]
    dynamic_update_slice x2 -> x8, other arithmetic: 27.3 us -> 40.2 us  [device_step(): lax.dynamic_update_slice(base, SHRINK * part, (jnp.int32(index * span), w...]
    reduce_scatter x3, waiting for transfers between devices: 31.6 us -> 44.4 us  [scatter_rows(): return lax.psum_scatter(values, ('z', 'y'), scatter_dimension=1, tiled=True)]
  transfers between devices with their start and end apart: 60 -> 63, of which waited for: 27 -> 27; matrix products, arithmetic and copies ran while one was open for 28% -> 30% of each run, Pallas kernels for 17% -> 16%
where the time goes in v2:
time: 1140 us
  waiting for transfers between devices  445 us (39%)
  Pallas kernels  196 us (17%)
  local copies, waits for them, and re-layouts  169 us (15%)
  other arithmetic  131 us (11%)
  matrix products  97.8 us (9%)
  starting transfers between devices  80 us (7%)
  between operations  16.1 us (1%)
    psum x1, waiting for transfers between devices, device_step(): d_table = lax.psum(d_table, ('z', 'y'))  172 us
    ppermute x1, waiting for transfers between devices, device_step(): lax.ppermute(d_rows, 'x', right)  67.5 us
    ppermute x3, waiting for transfers between devices, device_step(): lax.ppermute(top_sum, 'x', right)  61.4 us
    pallas_call x1, Pallas kernels, attention_backward(): pl.pallas_call(functools.partial(attn_bwd_kernel, seq_len // 2, rows), gr...  58.6 us
    dot_general x8, matrix products, dot(): return jnp.dot(left, right, preferred_element_type=F32)  49.5 us
    ppermute x5, waiting for transfers between devices, ring_blocks(): lax.ppermute(values, axis, right)  44.8 us
    reduce_scatter x3, waiting for transfers between devices, scatter_rows(): return lax.psum_scatter(values, ('z', 'y'), scatter_dimension=1, tiled=True)  44.4 us
    dynamic_update_slice x8, other arithmetic, device_step(): lax.dynamic_update_slice(base, SHRINK * part, (jnp.int32(index * span), w...  40.2 us
  transfers between devices with their start and end apart: 63, of which 27 were waited for; matrix products, arithmetic and copies ran while one was open for 30% of the time, Pallas kernels for 16%

profile of v2, /device:TPU:1, one launch (start us, length us, event | category | flops | bytes accessed | tf_op | source)
XLA Modules:
  0.0 1135.1 jit_solution(2768879802321702503)
XLA Ops:
  27.0 15.5 %gather_fusion = bf16[768,1024]{1,0:T(8,128)(2,1)S(1)} fusion(bf16[12576,1024]{1,0:T(8,128)(2,1)} %param.23, s32[1024]{0:T(1024)S(1)} %pad_clamp_fusion.2), kind=kCustom, calls=%fused_computation.4 | custom fusion | bytes 3148800 | tf_op jit(solution)/shard_map/gather | solution.py:476
  55.4 23.3 %gather_fusion.1 = bf16[2304,1024]{1,0:T(8,128)(2,1)} fusion(bf16[12576,1024]{1,0:T(8,128)(2,1)} %param.23, s32[3072]{0:T(1024)S(1)} %pad_clamp_fusion), kind=kCustom, calls=%fused_computation.5 | custom fusion | bytes 9446400 | tf_op jit(solution)/shard_map/gather | solution.py:495
  78.7 10.7 collective-permute-done.4
  89.4 3.9 fusion.15
  100.2 29.4 %collective-permute-done.5 = f32[384,1024]{1,0:T(8,128)S(1)} collective-permute-done((f32[384,1024]{1,0:T(8,128)}, f32[384,1024]{1,0:T(8,128)S(1)}, u32[]{:S(2)}, u32[]{:S(2)}) %collective-permute-start.5) | collective-permute-done | bytes 1572896 | tf_op jit(solution)/shard_map/ppermute | solution.py:508
  129.6 4.0 fusion.14
  141.7 6.2 fusion
  147.9 21.3 %collective-permute-done.6 = f32[384,1024]{1,0:T(8,128)} collective-permute-done((f32[384,1024]{1,0:T(8,128)}, f32[384,1024]{1,0:T(8,128)}, u32[]{:S(2)}, u32[]{:S(2)}) %collective-permute-start.6) | collective-permute-done | bytes 1572896 | tf_op jit(solution)/shard_map/ppermute | solution.py:508
  187.4 6.9 add_convert_fusion.qkv_ref
  194.4 33.5 %attn_fwd.1 = bf16[1536,512]{1,0:T(8,128)(2,1)S(1)} custom-call(s32[1]{0:T(128)} %bitcast.26.core_ref, bf16[1536,1536]{1,0:T(8,128)(2,1)} %add_convert_fusion.qkv_ref, f32[1536,128]{1,0:T(8,128)S(1)} %get-tuple-element.80.cos_ref, f32[1536,128]{1,0:T(8,128)S(1)} %get-tuple-element.81.sin_ref), custom_call_target="tpu_custom_call" | custom-call | flops 4831838208 | bytes 7077888 | tf_op jit(solution)/shard_map/attn_fwd/pallas_call | solution.py:162
  231.6 4.2 collective-permute-done.13
  259.8 25.7 %geglu_fwd.1 = (bf16[1536,2048]{1,0:T(8,128)(2,1)}, f32[1536,2048]{1,0:T(8,128)}, f32[1536,2048]{1,0:T(8,128)}, bf16[4096,1024]{1,0:T(8,128)(2,1)}) custom-call(bf16[1536,1024]{1,0:T(8,128)(2,1)} %pad_maximum_fusion.3.hidden_ref, f32[16,4,64,1024]{3,2,1,0:T(8,128)} %bitcast.312, f32[1,4096]{1,0:T(1,128)} %bitcast.301), custom_call_target="tpu_custom_call" | custom-call | flops 12884901888 | bytes 31457280 | tf_op jit(solution)/shard_map/geglu_fwd/pallas_call | solution.py:219
  288.3 8.2 fusion.5
  301.0 6.3 fusion.7
  319.5 5.7 collective-permute-done.19
  327.6 19.3 %geglu_bwd.1 = (bf16[1536,4096]{1,0:T(8,128)(2,1)}, f32[1,4096]{1,0:T(1,128)}) custom-call(bf16[1536,1024]{1,0:T(8,128)(2,1)} %pad_maximum_fusion.4.d_ffn_ref, bf16[2048,1024]{1,0:T(8,128)(2,1)} %bitcast.36.weight_ref, f32[1536,2048]{1,0:T(8,128)} %get-tuple-element.92.act_ref, f32[1536,2048]{1,0:T(8,128)} %get-tuple-element.93.slope_ref), custom_call_target="tpu_custom_call" | custom-call | flops 6442450944 | bytes 37748736 | tf_op jit(solution)/shard_map/geglu_bwd/pallas_call | solution.py:250
  346.9 12.0 %fusion.1 = f32[768,1024]{1,0:T(8,128)} fusion(bf16[4096,1024]{1,0:T(8,128)(2,1)} %get-tuple-element.95, bf16[1536,4096]{1,0:T(8,128)(2,1)} %get-tuple-element.94), kind=kOutput, calls=%fused_computation.19 | convolution fusion | flops 6442450944 | bytes 17825792 | tf_op jit(solution)/shard_map/dot_general | solution.py:40
  359.2 10.8 fusion.59
  370.1 11.0 fusion.3
  400.1 58.6 %attn_bwd.1 = (bf16[1536,1536]{1,0:T(8,128)(2,1)}, f32[1,1536]{1,0:T(1,128)}) custom-call(s32[1]{0:T(128)} %bitcast.26.core_ref, bf16[1536,1536]{1,0:T(8,128)(2,1)} %add_convert_fusion.qkv_ref, bf16[1536,512]{1,0:T(8,128)(2,1)} %convolution_convert_fusion.dctx_ref, f32[1536,128]{1,0:T(8,128)} %copy-done.6, f32[1536,128]{1,0:T(8,128)} %copy-done.7), custom_call_target="tpu_custom_call" | custom-call | flops 12079595520 | bytes 11796480 | tf_op jit(solution)/shard_map/attn_bwd/pallas_call | solution.py:182
  458.8 5.6 convolution_add_fusion
  467.8 4.4 convolution_add_fusion.1
  480.6 5.2 fusion.11
  485.7 4.8 pad_maximum_fusion
  490.9 20.6 %fusion.60 = f32[4096,1024]{1,0:T(8,128)} fusion(bf16[1536,4096]{1,0:T(8,128)(2,1)} %get-tuple-element.94, bf16[768,1024]{1,0:T(8,128)(2,1)} %copy-done.20, bf16[768,1024]{1,0:T(8,128)(2,1)} %copy-done.15), kind=kOutput, calls=%fused_computation.265 | convolution fusion | flops 12891193344 | bytes 32505856 | tf_op jit(solution)/shard_map/dot_general | solution.py:44
  514.3 67.5 %collective-permute-done.24.refs_1_ = f32[1536,512]{1,0:T(8,128)S(1)} collective-permute-done((f32[1536,512]{1,0:T(8,128)S(1)}, f32[1536,512]{1,0:T(8,128)S(1)}, u32[]{:S(2)}, u32[]{:S(2)}) %collective-permute-start.24) | collective-permute-done | bytes 3145760 | tf_op jit(solution)/shard_map/ppermute | solution.py:585
  588.9 31.5 %bucket_ids.1 = (s32[30720]{0:T(1024)}, s32[20]{0:T(128)}) custom-call(s32[6144]{0:T(1024)} %get-tuple-element.230.group_ref, s32[6144]{0:T(1024)} %get-tuple-element.229.value_ref), custom_call_target="tpu_custom_call" | custom-call | flops 40000000 | bytes 122880 | tf_op jit(solution)/shard_map/bucket_ids/pallas_call | solution.py:292
  623.9 27.1 %table_rows.1 = (f32[3144,512]{1,0:T(8,128)}, f32[3144,512]{1,0:T(8,128)}, f32[3144,512]{1,0:T(8,128)}, f32[3144,512]{1,0:T(8,128)}) custom-call(s32[30720]{0:T(1024)S(1)} %copy-done.8, s32[20]{0:T(128)S(1)} %copy-done.9, f32[1536,512]{1,0:T(8,128)S(1)} %maximum_add_fusion.refs_0_, f32[1536,512]{1,0:T(8,128)S(1)} %copy-done.3, f32[1536,512]{1,0:T(8,128)} %copy-done.19, ...), custom_call_target="tpu_custom_call" | custom-call | flops 193167360 | bytes 25755648 | tf_op jit(solution)/shard_map/table_rows/pallas_call | solution.py:363
  651.1 44.4 %reduce-scatter.6.cloned.1.call-done = f32[4,64,1024]{2,1,0:T(8,128)} async-done(((f32[4,1024,1024]{2,1,0:T(8,128)}), f32[4,64,1024]{2,1,0:T(8,128)}) %reduce-scatter.6.cloned.1.call-update) | async-done | bytes 1048592 | tf_op jit(solution)/shard_map/reduce_scatter | solution.py:557
  730.6 5.8 collective-permute-done.31
  736.5 10.7 collective-permute-done.33
  747.1 4.0 collective-permute-start.34
  761.7 35.1 %collective-permute-done.34 = f32[4,64,1024]{2,1,0:T(8,128)S(1)} collective-permute-done((f32[4,64,1024]{2,1,0:T(8,128)S(1)}, f32[4,64,1024]{2,1,0:T(8,128)S(1)}, u32[]{:S(2)}, u32[]{:S(2)}) %collective-permute-start.34) | collective-permute-done | bytes 1048608 | tf_op jit(solution)/shard_map/ppermute | solution.py:386
  808.1 14.3 %collective-permute-done.36 = f32[2,64,1024]{2,1,0:T(8,128)S(1)} collective-permute-done((f32[2,64,1024]{2,1,0:T(8,128)S(1)}, f32[2,64,1024]{2,1,0:T(8,128)S(1)}, u32[]{:S(2)}, u32[]{:S(2)}) %collective-permute-start.36) | collective-permute-done | bytes 524320 | tf_op jit(solution)/shard_map/ppermute | solution.py:389
  834.5 4.4 collective-permute-start.52
  842.7 4.9 broadcast_in_dim.309
  847.7 5.3 bitcast_dynamic-update-slice_fusion.1
  855.8 4.2 fusion.71
  860.0 5.5 copy.70
  865.5 5.3 copy.71
  870.8 5.2 bitcast_dynamic-update-slice_fusion
  879.2 6.8 slice.327
  888.0 171.9 %all-reduce.7.cloned.1.call-done = (f32[3144,512]{1,0:T(8,128)}, f32[3144,512]{1,0:T(8,128)}, f32[3144,512]{1,0:T(8,128)}, f32[3144,512]{1,0:T(8,128)}) async-done(((f32[3144,512]{1,0:T(8,128)}, f32[3144,512]{1,0:T(8,128)}, f32[3144,512]{1,0:T(8,128)}, f32[3144,512]{1,0:T(8,128)}), (f32[3144,512]{1,0:T(8,128)}, f32[3144,512]{1,0:T(8,128)}, f32[3144,512]{1,0:T(8,128)}, ...) | async-done | bytes 25755664 | tf_op jit(solution)/shard_map/psum | solution.py:613
  1070.9 16.9 %broadcast_in_dim.258 = f32[12576,1024]{1,0:T(8,128)} broadcast(f32[]{:T(128)} %constant.443.clone.1), dimensions={} | broadcast | bytes 51511300 | tf_op jit(solution)/shard_map/broadcast_in_dim | solution.py:643
  1087.8 6.6 multiply_dynamic-update-slice_fusion.7
  1094.4 6.6 multiply_dynamic-update-slice_fusion.6
  1108.1 6.4 multiply_dynamic-update-slice_fusion.3
  1114.5 6.4 multiply_dynamic-update-slice_fusion.2
  (447 shorter events, 265.0 us)
Async XLA Ops:
  7.2 130.8 %all-gather.3.cloned.1.call-start = ((), (), s32[]{:S(2)}) async-start(), calls=%async_computation.3 | async-start | bytes 11141120 | tf_op jit(solution)/shard_map/all_gather | solution.py:482
  17.5 25.0 %collective-permute-start.1 = (f32[104,1024]{1,0:T(8,128)S(1)}, f32[104,1024]{1,0:T(8,128)S(1)}, u32[]{:S(2)}, u32[]{:S(2)}) collective-permute-start(f32[104,1024]{1,0:T(8,128)S(1)} %pad_maximum_fusion.10), channel_id=1, source_target_pairs={{0,32},{32,64},{64,96},{96,0},{1,33},{33,65},{65,97},{97,1},{2,34}... | collective-permute-start | bytes 1277960 | tf_op jit(solution)/shard_map/ppermute | solution.py:386
  19.6 22.9 %collective-permute-start.2 = (f32[104,1024]{1,0:T(8,128)S(1)}, f32[104,1024]{1,0:T(8,128)S(1)}, u32[]{:S(2)}, u32[]{:S(2)}) collective-permute-start(f32[104,1024]{1,0:T(8,128)S(1)} %pad_maximum_fusion.10), channel_id=1, source_target_pairs={{0,96},{32,0},{64,32},{96,64},{1,97},{33,1},{65,33},{97,65},{2,98}... | collective-permute-start | bytes 1277960 | tf_op jit(solution)/shard_map/ppermute | solution.py:386
  20.9 23.1 %collective-permute-start.3 = (f32[104,1024]{1,0:T(8,128)S(1)}, f32[104,1024]{1,0:T(8,128)}, u32[]{:S(2)}, u32[]{:S(2)}) collective-permute-start(f32[104,1024]{1,0:T(8,128)S(1)} %pad_maximum_fusion.10), channel_id=1, source_target_pairs={{0,64},{32,96},{64,0},{96,32},{1,65},{33,97},{65,1},{97,33},{2,66}... | collective-permute-start | bytes 1277960 | tf_op jit(solution)/shard_map/ppermute | solution.py:391
  48.3 211.5 %all-gather.5.cloned.1.call-start = ((), (), s32[]{:S(2)}) async-start(), calls=%async_computation.4 | async-start | bytes 17825792 | tf_op jit(solution)/shard_map/all_gather | solution.py:482
  49.4 601.6 %reduce-scatter.4.cloned.1.call-start = ((), (), s32[]{:S(2)}) async-start(), calls=%async_computation.5 | async-start | bytes 8912896 | tf_op jit(solution)/shard_map/reduce_scatter | solution.py:557
  52.2 37.1 %collective-permute-start.4 = (f32[384,1024]{1,0:T(8,128)}, f32[384,1024]{1,0:T(8,128)S(1)}, u32[]{:S(2)}, u32[]{:S(2)}) collective-permute-start(f32[384,1024]{1,0:T(8,128)} %get-tuple-element.212), channel_id=1, source_target_pairs={{0,32},{32,64},{64,96},{96,0},{1,33},{33,65},{65,97},{97,1},{2,34}... | collective-permute-start | bytes 4718600 | tf_op jit(solution)/shard_map/ppermute | solution.py:508
  52.5 36.8 %collective-permute-start.7 = (f32[384,1024]{1,0:T(8,128)S(1)}, f32[384,1024]{1,0:T(8,128)}, u32[]{:S(2)}, u32[]{:S(2)}) collective-permute-start(f32[384,1024]{1,0:T(8,128)S(1)} %get-tuple-element.211), channel_id=1, source_target_pairs={{0,96},{32,0},{64,32},{96,64},{1,97},{33,1},{65,33},{97,65},{2,98}... | collective-permute-start | bytes 4718600 | tf_op jit(solution)/shard_map/ppermute | solution.py:508
  93.3 36.3 %collective-permute-start.5 = (f32[384,1024]{1,0:T(8,128)}, f32[384,1024]{1,0:T(8,128)S(1)}, u32[]{:S(2)}, u32[]{:S(2)}) collective-permute-start(f32[384,1024]{1,0:T(8,128)} %get-tuple-element.205), channel_id=1, source_target_pairs={{0,32},{32,64},{64,96},{96,0},{1,33},{33,65},{65,97},{97,1},{2,34}... | collective-permute-start | bytes 4718600 | tf_op jit(solution)/shard_map/ppermute | solution.py:508
  93.3 36.3 %collective-permute-start.8 = (f32[384,1024]{1,0:T(8,128)}, f32[384,1024]{1,0:T(8,128)}, u32[]{:S(2)}, u32[]{:S(2)}) collective-permute-start(f32[384,1024]{1,0:T(8,128)} %get-tuple-element.204), channel_id=1, source_target_pairs={{0,96},{32,0},{64,32},{96,64},{1,97},{33,1},{65,33},{97,65},{2,98}... | collective-permute-start | bytes 4718600 | tf_op jit(solution)/shard_map/ppermute | solution.py:508
  133.6 35.6 %collective-permute-start.6 = (f32[384,1024]{1,0:T(8,128)}, f32[384,1024]{1,0:T(8,128)}, u32[]{:S(2)}, u32[]{:S(2)}) collective-permute-start(f32[384,1024]{1,0:T(8,128)} %get-tuple-element.203), channel_id=1, source_target_pairs={{0,32},{32,64},{64,96},{96,0},{1,33},{33,65},{65,97},{97,1},{2,34}... | collective-permute-start | bytes 4718600 | tf_op jit(solution)/shard_map/ppermute | solution.py:508
  134.1 35.1 %collective-permute-start.9 = (f32[384,1024]{1,0:T(8,128)}, f32[384,1024]{1,0:T(8,128)}, u32[]{:S(2)}, u32[]{:S(2)}) collective-permute-start(f32[384,1024]{1,0:T(8,128)} %get-tuple-element.202), channel_id=1, source_target_pairs={{0,96},{32,0},{64,32},{96,64},{1,97},{33,1},{65,33},{97,65},{2,98}... | collective-permute-start | bytes 4718600 | tf_op jit(solution)/shard_map/ppermute | solution.py:508
  179.5 48.7 %collective-permute-start.11 = (f32[512,1024]{1,0:T(8,128)}, f32[512,1024]{1,0:T(8,128)}, u32[]{:S(2)}, u32[]{:S(2)}) collective-permute-start(f32[512,1024]{1,0:T(8,128)} %dynamic-slice_convert_fusion), channel_id=1, source_target_pairs={{0,32},{32,64},{64,96},{96,0},{1,33},{33,65},{65,97},{97,1},{2,34}... | collective-permute-start | bytes 6291464 | tf_op jit(solution)/shard_map/ppermute | solution.py:518
  180.4 47.8 %collective-permute-start.12 = (f32[512,1024]{1,0:T(8,128)}, f32[512,1024]{1,0:T(8,128)}, u32[]{:S(2)}, u32[]{:S(2)}) collective-permute-start(f32[512,1024]{1,0:T(8,128)} %dynamic-slice_convert_fusion), channel_id=1, source_target_pairs={{0,96},{32,0},{64,32},{96,64},{1,97},{33,1},{65,33},{97,65},{2,98}... | collective-permute-start | bytes 6291464 | tf_op jit(solution)/shard_map/ppermute | solution.py:518
  237.5 18.7 %collective-permute-start.14 = (f32[768,1024]{1,0:T(8,128)S(1)}, f32[768,1024]{1,0:T(8,128)S(1)}, u32[]{:S(2)}, u32[]{:S(2)}) collective-permute-start(f32[768,1024]{1,0:T(8,128)S(1)} %get-tuple-element.186), channel_id=1, source_target_pairs={{0,1},{1,0},{2,3},{3,2},{4,5},{5,4},{6,7},{7,6},{8,9},{9,8},{10,11... | collective-permute-start | bytes 9437192 | tf_op jit(solution)/shard_map/ppermute | solution.py:21
  245.7 39.9 %collective-permute-start.15 = (f32[256,1024]{1,0:T(8,128)}, f32[256,1024]{1,0:T(8,128)}, u32[]{:S(2)}, u32[]{:S(2)}) collective-permute-start(f32[256,1024]{1,0:T(8,128)} %slice.242), channel_id=1, source_target_pairs={{0,32},{32,64},{64,96},{96,0},{1,33},{33,65},{65,97},{97,1},{2,34}... | collective-permute-start | bytes 3145736 | tf_op jit(solution)/shard_map/ppermute | solution.py:540
  249.1 36.5 %collective-permute-start.16 = (f32[256,1024]{1,0:T(8,128)}, f32[256,1024]{1,0:T(8,128)}, u32[]{:S(2)}, u32[]{:S(2)}) collective-permute-start(f32[256,1024]{1,0:T(8,128)} %slice.243), channel_id=1, source_target_pairs={{0,96},{32,0},{64,32},{96,64},{1,97},{33,1},{65,33},{97,65},{2,98}... | collective-permute-start | bytes 3145736 | tf_op jit(solution)/shard_map/ppermute | solution.py:540
  358.9 22.3 %collective-permute-start.20 = (f32[768,1024]{1,0:T(8,128)}, f32[768,1024]{1,0:T(8,128)}, u32[]{:S(2)}, u32[]{:S(2)}) collective-permute-start(f32[768,1024]{1,0:T(8,128)} %fusion.1), channel_id=1, source_target_pairs={{0,1},{1,0},{2,3},{3,2},{4,5},{5,4},{6,7},{7,6},{8,9},{9,8},{10,11... | collective-permute-start | bytes 9437192 | tf_op jit(solution)/shard_map/ppermute | solution.py:21
  370.1 281.0 %reduce-scatter.8.cloned.1.call-start = ((), (), s32[]{:S(2)}) async-start(), calls=%async_computation.7 | async-start | bytes 11141120 | tf_op jit(solution)/shard_map/reduce_scatter | solution.py:557
  490.6 204.9 %reduce-scatter.6.cloned.1.call-start = ((), (), s32[]{:S(2)}) async-start(), calls=%async_computation.6 | async-start | bytes 17825792 | tf_op jit(solution)/shard_map/reduce_scatter | solution.py:557
  511.5 548.4 %all-reduce.7.cloned.1.call-start = ((), (), s32[]{:S(2)}) async-start(), calls=%async_computation.8 | async-start | bytes 51511296 | tf_op jit(solution)/shard_map/psum | solution.py:613
  511.5 70.3 %collective-permute-start.24 = (f32[1536,512]{1,0:T(8,128)S(1)}, f32[1536,512]{1,0:T(8,128)S(1)}, u32[]{:S(2)}, u32[]{:S(2)}) collective-permute-start(f32[1536,512]{1,0:T(8,128)S(1)} %maximum_add_fusion.refs_0_), channel_id=1, source_target_pairs={{0,32},{32,64},{64,96},{96,0},{1,33},{33,65},{65,97},{97,1},{2,34}... | collective-permute-start | bytes 9437192 | tf_op jit(solution)/shard_map/ppermute | solution.py:585
  511.8 71.4 %collective-permute-start.25 = (f32[1536,512]{1,0:T(8,128)S(1)}, f32[1536,512]{1,0:T(8,128)S(1)}, u32[]{:S(2)}, u32[]{:S(2)}) collective-permute-start(f32[1536,512]{1,0:T(8,128)S(1)} %maximum_add_fusion.refs_0_), channel_id=1, source_target_pairs={{0,96},{32,0},{64,32},{96,64},{1,97},{33,1},{65,33},{97,65},{2,98}... | collective-permute-start | bytes 9437192 | tf_op jit(solution)/shard_map/ppermute | solution.py:585
  583.2 37.1 %collective-permute-start.26 = (f32[768,512]{1,0:T(8,128)}, f32[768,512]{1,0:T(8,128)}, u32[]{:S(2)}, u32[]{:S(2)}) collective-permute-start(f32[768,512]{1,0:T(8,128)} %slice.319), channel_id=1, source_target_pairs={{0,32},{32,64},{64,96},{96,0},{1,33},{33,65},{65,97},{97,1},{2,34}... | collective-permute-start | bytes 4718600 | tf_op jit(solution)/shard_map/ppermute | solution.py:608
  584.7 35.6 %collective-permute-start.27 = (f32[768,512]{1,0:T(8,128)}, f32[768,512]{1,0:T(8,128)}, u32[]{:S(2)}, u32[]{:S(2)}) collective-permute-start(f32[768,512]{1,0:T(8,128)} %slice.320), channel_id=1, source_target_pairs={{0,96},{32,0},{64,32},{96,64},{1,97},{33,1},{65,33},{97,65},{2,98}... | collective-permute-start | bytes 4718600 | tf_op jit(solution)/shard_map/ppermute | solution.py:609
  705.3 13.5 %collective-permute-start.28 = (f32[64,1024]{1,0:T(8,128)S(1)}, f32[64,1024]{1,0:T(8,128)S(1)}, u32[]{:S(2)}, u32[]{:S(2)}) collective-permute-start(f32[64,1024]{1,0:T(8,128)S(1)} %get-tuple-element.220), channel_id=1, source_target_pairs={{0,32},{32,64},{64,96},{96,0},{1,33},{33,65},{65,97},{97,1},{2,34}... | collective-permute-start | bytes 786440 | tf_op jit(solution)/shard_map/ppermute | solution.py:602
  705.8 18.1 %collective-permute-start.29 = (f32[64,1024]{1,0:T(8,128)S(1)}, f32[64,1024]{1,0:T(8,128)S(1)}, u32[]{:S(2)}, u32[]{:S(2)}) collective-permute-start(f32[64,1024]{1,0:T(8,128)S(1)} %get-tuple-element.222), channel_id=1, source_target_pairs={{0,64},{32,96},{64,0},{96,32},{1,65},{33,97},{65,1},{97,33},{2,66}... | collective-permute-start | bytes 786440 | tf_op jit(solution)/shard_map/ppermute | solution.py:602
  709.0 14.8 %collective-permute-start.30 = (f32[64,1024]{1,0:T(8,128)S(1)}, f32[64,1024]{1,0:T(8,128)S(1)}, u32[]{:S(2)}, u32[]{:S(2)}) collective-permute-start(f32[64,1024]{1,0:T(8,128)S(1)} %get-tuple-element.221), channel_id=1, source_target_pairs={{0,96},{32,0},{64,32},{96,64},{1,97},{33,1},{65,33},{97,65},{2,98}... | collective-permute-start | bytes 786440 | tf_op jit(solution)/shard_map/ppermute | solution.py:602
  712.8 14.8 %collective-permute-start.45 = (f32[72,1024]{1,0:T(8,128)S(1)}, f32[72,1024]{1,0:T(8,128)S(1)}, u32[]{:S(2)}, u32[]{:S(2)}) collective-permute-start(f32[72,1024]{1,0:T(8,128)S(1)} %pad_maximum_fusion.11), channel_id=1, source_target_pairs={{0,2},{2,4},{4,6},{6,0},{1,3},{3,5},{5,7},{7,1},{8,10},{10,12},{12... | collective-permute-start | bytes 884744 | tf_op jit(solution)/shard_map/ppermute | solution.py:386
  714.1 37.4 %collective-permute-start.46 = (f32[72,1024]{1,0:T(8,128)S(1)}, f32[72,1024]{1,0:T(8,128)S(1)}, u32[]{:S(2)}, u32[]{:S(2)}) collective-permute-start(f32[72,1024]{1,0:T(8,128)S(1)} %pad_maximum_fusion.11), channel_id=1, source_target_pairs={{0,6},{2,0},{4,2},{6,4},{1,7},{3,1},{5,3},{7,5},{8,14},{10,8},{12,... | collective-permute-start | bytes 884744 | tf_op jit(solution)/shard_map/ppermute | solution.py:386
  718.8 32.7 %collective-permute-start.47 = (f32[72,1024]{1,0:T(8,128)S(1)}, f32[72,1024]{1,0:T(8,128)S(1)}, u32[]{:S(2)}, u32[]{:S(2)}) collective-permute-start(f32[72,1024]{1,0:T(8,128)S(1)} %pad_maximum_fusion.11), channel_id=1, source_target_pairs={{0,4},{2,6},{4,0},{6,2},{1,5},{3,7},{5,1},{7,3},{8,12},{10,14},{12... | collective-permute-start | bytes 884744 | tf_op jit(solution)/shard_map/ppermute | solution.py:391
  724.0 12.4 %collective-permute-start.31 = (f32[64,1024]{1,0:T(8,128)S(1)}, f32[64,1024]{1,0:T(8,128)S(1)}, u32[]{:S(2)}, u32[]{:S(2)}) collective-permute-start(f32[64,1024]{1,0:T(8,128)S(1)} %get-tuple-element.170), channel_id=1, source_target_pairs={{0,8},{8,16},{16,24},{24,0},{1,9},{9,17},{17,25},{25,1},{2,10},{10... | collective-permute-start | bytes 786440 | tf_op jit(solution)/shard_map/ppermute | solution.py:386
  725.5 10.9 collective-permute-start.32
  727.6 19.5 %collective-permute-start.33 = (f32[64,1024]{1,0:T(8,128)S(1)}, f32[64,1024]{1,0:T(8,128)S(1)}, u32[]{:S(2)}, u32[]{:S(2)}) collective-permute-start(f32[64,1024]{1,0:T(8,128)S(1)} %get-tuple-element.170), channel_id=1, source_target_pairs={{0,16},{8,24},{16,0},{24,8},{1,17},{9,25},{17,1},{25,9},{2,18},{10... | collective-permute-start | bytes 786440 | tf_op jit(solution)/shard_map/ppermute | solution.py:391
  747.1 49.7 %collective-permute-start.34 = (f32[4,64,1024]{2,1,0:T(8,128)S(1)}, f32[4,64,1024]{2,1,0:T(8,128)S(1)}, u32[]{:S(2)}, u32[]{:S(2)}) collective-permute-start(f32[4,64,1024]{2,1,0:T(8,128)S(1)} %bitcast_dynamic-update-slice_fusion.17), channel_id=1, source_target_pairs={{0,2},{2,4},{4,6},{6,0},{1,3},{3,5},{5,7},{7,1},{8,10},{10,12},{12... | collective-permute-start | bytes 3145736 | tf_op jit(solution)/shard_map/ppermute | solution.py:386
  751.2 47.1 %collective-permute-start.35 = (f32[4,64,1024]{2,1,0:T(8,128)S(1)}, f32[4,64,1024]{2,1,0:T(8,128)S(1)}, u32[]{:S(2)}, u32[]{:S(2)}) collective-permute-start(f32[4,64,1024]{2,1,0:T(8,128)S(1)} %bitcast_dynamic-update-slice_fusion.17), channel_id=1, source_target_pairs={{0,6},{2,0},{4,2},{6,4},{1,7},{3,1},{5,3},{7,5},{8,14},{10,8},{12,... | collective-permute-start | bytes 3145736 | tf_op jit(solution)/shard_map/ppermute | solution.py:386
  751.5 53.7 %collective-permute-start.48 = (f32[4,72,1024]{2,1,0:T(8,128)S(1)}, f32[4,72,1024]{2,1,0:T(8,128)S(1)}, u32[]{:S(2)}, u32[]{:S(2)}) collective-permute-start(f32[4,72,1024]{2,1,0:T(8,128)S(1)} %bitcast_dynamic-update-slice_fusion.13), channel_id=1, source_target_pairs={{0,8},{8,16},{16,24},{24,0},{1,9},{9,17},{17,25},{25,1},{2,10},{10... | collective-permute-start | bytes 3538952 | tf_op jit(solution)/shard_map/ppermute | solution.py:386
  752.2 53.2 %collective-permute-start.49 = (f32[4,72,1024]{2,1,0:T(8,128)S(1)}, f32[4,72,1024]{2,1,0:T(8,128)S(1)}, u32[]{:S(2)}, u32[]{:S(2)}) collective-permute-start(f32[4,72,1024]{2,1,0:T(8,128)S(1)} %bitcast_dynamic-update-slice_fusion.13), channel_id=1, source_target_pairs={{0,24},{8,0},{16,8},{24,16},{1,25},{9,1},{17,9},{25,17},{2,26},{10... | collective-permute-start | bytes 3538952 | tf_op jit(solution)/shard_map/ppermute | solution.py:386
  796.9 25.5 %collective-permute-start.36 = (f32[2,64,1024]{2,1,0:T(8,128)S(1)}, f32[2,64,1024]{2,1,0:T(8,128)S(1)}, u32[]{:S(2)}, u32[]{:S(2)}) collective-permute-start(f32[2,64,1024]{2,1,0:T(8,128)S(1)} %slice.321), channel_id=1, source_target_pairs={{0,2},{2,4},{4,6},{6,0},{1,3},{3,5},{5,7},{7,1},{8,10},{10,12},{12... | collective-permute-start | bytes 1572872 | tf_op jit(solution)/shard_map/ppermute | solution.py:389
  798.4 24.3 %collective-permute-start.37 = (f32[2,64,1024]{2,1,0:T(8,128)S(1)}, f32[2,64,1024]{2,1,0:T(8,128)S(1)}, u32[]{:S(2)}, u32[]{:S(2)}) collective-permute-start(f32[2,64,1024]{2,1,0:T(8,128)S(1)} %slice.322), channel_id=1, source_target_pairs={{0,6},{2,0},{4,2},{6,4},{1,7},{3,1},{5,3},{7,5},{8,14},{10,8},{12,... | collective-permute-start | bytes 1572872 | tf_op jit(solution)/shard_map/ppermute | solution.py:389
  805.3 28.2 %collective-permute-start.50 = (f32[2,72,1024]{2,1,0:T(8,128)S(1)}, f32[2,72,1024]{2,1,0:T(8,128)S(1)}, u32[]{:S(2)}, u32[]{:S(2)}) collective-permute-start(f32[2,72,1024]{2,1,0:T(8,128)S(1)} %slice.325), channel_id=1, source_target_pairs={{0,8},{8,16},{16,24},{24,0},{1,9},{9,17},{17,25},{25,1},{2,10},{10... | collective-permute-start | bytes 1769480 | tf_op jit(solution)/shard_map/ppermute | solution.py:389
  805.4 28.0 %collective-permute-start.51 = (f32[2,72,1024]{2,1,0:T(8,128)S(1)}, f32[2,72,1024]{2,1,0:T(8,128)S(1)}, u32[]{:S(2)}, u32[]{:S(2)}) collective-permute-start(f32[2,72,1024]{2,1,0:T(8,128)S(1)} %slice.326), channel_id=1, source_target_pairs={{0,24},{8,0},{16,8},{24,16},{1,25},{9,1},{17,9},{25,17},{2,26},{10... | collective-permute-start | bytes 1769480 | tf_op jit(solution)/shard_map/ppermute | solution.py:389
  823.7 29.3 %collective-permute-start.38 = (f32[16,64,1024]{2,1,0:T(8,128)}, f32[16,64,1024]{2,1,0:T(8,128)}, u32[]{:S(2)}, u32[]{:S(2)}) collective-permute-start(f32[16,64,1024]{2,1,0:T(8,128)} %bitcast.59), channel_id=1, source_target_pairs={{0,1},{1,0},{2,3},{3,2},{4,5},{5,4},{6,7},{7,6},{8,9},{9,8},{10,11... | collective-permute-start | bytes 12582920 | tf_op jit(solution)/shard_map/ppermute | solution.py:21
  834.5 36.4 %collective-permute-start.52 = (f32[16,72,1024]{2,1,0:T(8,128)}, f32[16,72,1024]{2,1,0:T(8,128)}, u32[]{:S(2)}, u32[]{:S(2)}) collective-permute-start(f32[16,72,1024]{2,1,0:T(8,128)} %bitcast.83), channel_id=1, source_target_pairs={{0,1},{1,0},{2,3},{3,2},{4,5},{5,4},{6,7},{7,6},{8,9},{9,8},{10,11... | collective-permute-start | bytes 14155784 | tf_op jit(solution)/shard_map/ppermute | solution.py:21
  1059.9 48.2 %collective-permute-start.53 = (f32[3144,512]{1,0:T(8,128)}, f32[3144,512]{1,0:T(8,128)}, u32[]{:S(2)}, u32[]{:S(2)}) collective-permute-start(f32[3144,512]{1,0:T(8,128)} %get-tuple-element.115), channel_id=1, source_target_pairs={{0,1},{1,0},{2,3},{3,2},{4,5},{5,4},{6,7},{7,6},{8,9},{9,8},{10,11... | collective-permute-start | bytes 19316744 | tf_op jit(solution)/shard_map/ppermute | solution.py:21
  1070.1 44.4 %collective-permute-start.54 = (f32[3144,512]{1,0:T(8,128)}, f32[3144,512]{1,0:T(8,128)}, u32[]{:S(2)}, u32[]{:S(2)}) collective-permute-start(f32[3144,512]{1,0:T(8,128)} %get-tuple-element.116), channel_id=1, source_target_pairs={{0,1},{1,0},{2,3},{3,2},{4,5},{5,4},{6,7},{7,6},{8,9},{9,8},{10,11... | collective-permute-start | bytes 19316744 | tf_op jit(solution)/shard_map/ppermute | solution.py:21
  1070.1 50.8 %collective-permute-start.55 = (f32[3144,512]{1,0:T(8,128)}, f32[3144,512]{1,0:T(8,128)S(1)}, u32[]{:S(2)}, u32[]{:S(2)}) collective-permute-start(f32[3144,512]{1,0:T(8,128)} %get-tuple-element.117), channel_id=1, source_target_pairs={{0,1},{1,0},{2,3},{3,2},{4,5},{5,4},{6,7},{7,6},{8,9},{9,8},{10,11... | collective-permute-start | bytes 19316744 | tf_op jit(solution)/shard_map/ppermute | solution.py:21
  1070.6 53.8 %collective-permute-start.56 = (f32[3144,512]{1,0:T(8,128)}, f32[3144,512]{1,0:T(8,128)S(1)}, u32[]{:S(2)}, u32[]{:S(2)}) collective-permute-start(f32[3144,512]{1,0:T(8,128)} %get-tuple-element.118), channel_id=1, source_target_pairs={{0,1},{1,0},{2,3},{3,2},{4,5},{5,4},{6,7},{7,6},{8,9},{9,8},{10,11... | collective-permute-start | bytes 19316744 | tf_op jit(solution)/shard_map/ppermute | solution.py:21
  (78 other events, 1037.4 us)
Sparse Core Ops, SparseCore 0:
  48.4 81.0 all-gather.2
  131.6 110.9 all-gather.4
  370.2 85.1 reduce-scatter.3
  490.7 90.0 reduce-scatter.7
  584.6 110.8 reduce-scatter.5
  699.7 360.1 all-reduce.6
